TPU v7x, 512 devices: a whole 4x8x8 slice. The times are simulated.
512 devices in a mesh: blk: 128 (over y, x, z_hi), sub: 4 (over z_lo, core).
Axes of the slice: x: 4, y: 8, z: 8 (z_hi: 4, z_lo: 2; z = z_hi * 2 + z_lo), core: 2. Of those that a mesh axis runs over, the one named last changes fastest.
Arguments:
- first_core: bfloat16 [128, 128], P('blk'), may hold values from -6 to 6
- middle_core: bfloat16 [32, 32, 256], P(None, 'sub'), may hold values from -1 to 1
- last_core: bfloat16 [32, 512], replicated, may hold values from -1 to 1
- row_tt: int32 [524288], P(('blk', 'sub')), may hold values from 0 to 524287, as said below
Outputs:
- served: bfloat16 [524288, 128], P(('blk', 'sub'))
Inputs may be any that keep to these rules, and one draw needn't show every extreme that they name: `row_tt`: each window row is named exactly once. Among the rows of one device, exactly 2 entries lie in each of the 512 ranges q * 1024 to (q + 1) * 1024 - 1.
All inputs are finite; a program needn't handle non-finite values.
Results may differ from a plain program's by a relative error of at most 0.0049.
Values may be sent and summed in bfloat16 or wider, within the bound.
No kernel may reach another device: no remote copies, remote signals or barrier semaphores. Data moves between devices by JAX's collectives and lax.ppermute only.
A program may use at most 64 MiB of HBM per device.

v0:
```python
import jax
import jax.numpy as jnp
from jax import lax
from jax.sharding import PartitionSpec as P

R = 32
J1 = 4
J2 = 8
J3 = 4


def on_device(first_core, middle_core, last_core, row_tt):
    blocks = lax.axis_size("blk")
    groups = lax.axis_size("sub")
    sources = blocks * groups
    rows_here = row_tt.shape[0]
    per_peer = rows_here // sources
    row_width = J1 * J2 * J3
    last_span = last_core.shape[1] // J3
    middle_span = middle_core.shape[1]
    first_mat = first_core.reshape(J1, R)
    partial_value = jnp.dot(
        first_mat, middle_core.reshape(R, middle_span * J2 * R), preferred_element_type=jnp.float32
    ).astype(jnp.bfloat16)
    partial_value = (
        partial_value.reshape(J1, middle_span, J2, R)
        .transpose(1, 0, 2, 3)
        .reshape(middle_span * J1 * J2, R)
    )
    products = jnp.dot(partial_value, last_core, preferred_element_type=jnp.float32).astype(
        jnp.bfloat16
    )
    products = products.reshape(middle_span, J1, J2, last_span, J3).transpose(0, 3, 1, 2, 4)
    slab_table = products.reshape(middle_span * last_span, row_width)
    owners = row_tt // rows_here
    item_index = row_tt % rows_here
    row_order = jnp.argsort(owners, stable=True)
    wanted = item_index[row_order].reshape(blocks, groups, per_peer)
    asked_rows = lax.all_to_all(
        lax.all_to_all(wanted, "blk", split_axis=0, concat_axis=0, tiled=True),
        "sub",
        split_axis=1,
        concat_axis=1,
        tiled=True,
    )
    picked = jnp.take(slab_table, asked_rows.reshape(-1), axis=0).reshape(
        blocks, groups, per_peer, row_width
    )
    arrived = lax.all_to_all(
        lax.all_to_all(picked, "blk", split_axis=0, concat_axis=0, tiled=True),
        "sub",
        split_axis=1,
        concat_axis=1,
        tiled=True,
    )
    gathered = arrived.reshape(rows_here, row_width)
    return jnp.take(gathered, jnp.argsort(row_order), axis=0)


def solution(mesh):
    placed = (P("blk", None), P(None, "sub", None), P(), P(("blk", "sub")))
    return jax.shard_map(
        on_device, mesh=mesh, in_specs=placed, out_specs=P(("blk", "sub"), None), check_vma=False
    )
```

profile of v0, /device:TPU:1, one launch (start us, length us, event | category | flops | bytes accessed | tf_op | source)
XLA Modules:
  0.0 107.4 jit_solution(1154487396162525174)
XLA Ops:
  0.0 0.7 add_select_fusion
  0.7 4.4 %sort.34 = (s32[1024]{0:T(1024)}, s32[1024]{0:T(1024)S(1)}) sort(s32[1024]{0:T(1024)S(1)} %get-tuple-element.10, s32[1024]{0:T(1024)S(1)} %iota.8), dimensions={0}, to_apply=%region_0.1 | sort | flops 10240 | bytes 16384 | tf_op jit(solution)/shard_map/jit(argsort)/sort | solution.py:37
  5.1 4.5 %gather_fusion = s32[1024]{0:T(1024)S(1)} fusion(s32[1024]{0:T(1024)S(1)} %get-tuple-element.11, s32[1024]{0:T(1024)S(1)} %fusion), kind=kCustom, calls=%fused_computation.2 | custom fusion | bytes 12288 | tf_op jit(solution)/shard_map/gather | solution.py:38
  9.6 0.3 reshape.41
  10.0 1.5 %copy.19 = s32[128,4,2]{1,2,0:T(2,128)} copy(s32[128,4,2]{2,1,0:T(4,128)S(1)} %reshape.41) | data formatting | bytes 8192 | tf_op jit(solution)/shard_map/reshape | solution.py:38
  11.5 20.8 %all-to-all-start = ((s32[128,4,2]{1,2,0:T(2,128)}), s32[128,4,2]{1,2,0:T(2,128)S(1)}, u32[]{:S(2)}, u32[]{:S(2)}) async-start(s32[128,4,2]{1,2,0:T(2,128)} %copy.19), calls=%async_computation | async-start | bytes 262144 | tf_op jit(solution)/shard_map/all_to_all | solution.py:40
  32.3 0.6 broadcast.37
  32.9 0.7 reduce.3
  34.0 11.9 %all-to-all-done = s32[128,4,2]{1,2,0:T(2,128)S(1)} async-done(((s32[128,4,2]{1,2,0:T(2,128)}), s32[128,4,2]{1,2,0:T(2,128)S(1)}, u32[]{:S(2)}, u32[]{:S(2)}) %all-to-all-start) | async-done | bytes 4128 | tf_op jit(solution)/shard_map/all_to_all | solution.py:40
  45.9 0.7 copy.20
  46.6 5.3 %all-to-all-start.1 = ((s32[128,4,2]{0,2,1:T(2,128)}), s32[128,4,2]{0,2,1:T(2,128)S(1)}, u32[]{:S(2)}, u32[]{:S(2)}) async-start(s32[128,4,2]{0,2,1:T(2,128)} %copy.20), calls=%async_computation.1 | async-start | bytes 8192 | tf_op jit(solution)/shard_map/all_to_all | solution.py:39
  52.3 5.9 %reshape.39 = bf16[8,4,8,128,4]{2,1,0,4,3:T(4,128)(2,1)} reshape(bf16[256,512]{0,1:T(8,128)(2,1)S(1)} %copy.23) | data formatting | bytes 524288 | tf_op jit(solution)/shard_map/reshape | solution.py:33
  58.2 6.1 %copy.24 = bf16[8,128,4,8,4]{1,0,4,3,2:T(8,128)(2,1)S(1)} copy(bf16[8,128,4,8,4]{3,2,0,4,1:T(4,128)(2,1)} %bitcast.22) | data formatting | bytes 524288 | tf_op jit(solution)/shard_map/transpose | solution.py:33
  64.7 0.2 reshape.42
  65.0 3.2 %gather_fusion.1 = bf16[1024,128]{1,0:T(8,128)(2,1)S(1)} fusion(bf16[1024,128]{1,0:T(8,128)(2,1)S(1)} %copy.25, s32[1024]{0:T(1024)S(1)} %fusion.2), kind=kCustom, calls=%fused_computation.clone | custom fusion | bytes 528384 | tf_op jit(solution)/shard_map/jit(_take)/gather | solution.py:46
  68.2 0.9 broadcast_select_fusion.1
  69.1 6.2 %all-to-all-start.2 = ((bf16[128,4,2,128]{3,2,1,0:T(2,128)(2,1)}), bf16[128,4,2,128]{3,2,1,0:T(2,128)(2,1)S(1)}, u32[]{:S(2)}, u32[]{:S(2)}) async-start(bf16[128,4,2,128]{3,2,1,0:T(2,128)(2,1)} %bitcast.3), calls=%async_computation.2 | async-start | bytes 524288 | tf_op jit(solution)/shard_map/all_to_all | solution.py:50
  75.3 4.4 %sort.35 = (s32[1024]{0:T(1024)}, s32[1024]{0:T(1024)S(1)}) sort(s32[1024]{0:T(1024)S(1)} %get-tuple-element.8, s32[1024]{0:T(1024)S(1)} %iota.9), dimensions={0}, to_apply=%region_1.3 | sort | flops 10240 | bytes 16384 | tf_op jit(solution)/shard_map/jit(argsort)/sort | solution.py:57
  79.6 12.3 %all-to-all-done.2 = bf16[128,4,2,128]{3,2,1,0:T(2,128)(2,1)S(1)} async-done(((bf16[128,4,2,128]{3,2,1,0:T(2,128)(2,1)}), bf16[128,4,2,128]{3,2,1,0:T(2,128)(2,1)S(1)}, u32[]{:S(2)}, u32[]{:S(2)}) %all-to-all-start.2) | async-done | bytes 262176 | tf_op jit(solution)/shard_map/all_to_all | solution.py:50
  91.9 0.9 copy.26
  92.8 5.2 %all-to-all-start.3 = ((bf16[128,4,2,128]{3,2,0,1:T(2,128)(2,1)}), bf16[128,4,2,128]{3,2,0,1:T(2,128)(2,1)S(1)}, u32[]{:S(2)}, u32[]{:S(2)}) async-start(bf16[128,4,2,128]{3,2,0,1:T(2,128)(2,1)} %copy.26), calls=%async_computation.3 | async-start | bytes 524288 | tf_op jit(solution)/shard_map/all_to_all | solution.py:49
  98.0 5.0 %all-to-all-done.3 = bf16[128,4,2,128]{3,2,0,1:T(2,128)(2,1)S(1)} async-done(((bf16[128,4,2,128]{3,2,0,1:T(2,128)(2,1)}), bf16[128,4,2,128]{3,2,0,1:T(2,128)(2,1)S(1)}, u32[]{:S(2)}, u32[]{:S(2)}) %all-to-all-start.3) | async-done | bytes 262176 | tf_op jit(solution)/shard_map/all_to_all | solution.py:49
  103.3 3.2 %gather_fusion.2 = bf16[1024,128]{1,0:T(8,128)(2,1)S(1)} fusion(bf16[1024,128]{1,0:T(8,128)(2,1)S(1)} %bitcast.21, s32[1024]{0:T(1024)S(1)} %fusion.3), kind=kCustom, calls=%fused_computation.1.clone | custom fusion | bytes 528384 | tf_op jit(solution)/shard_map/jit(_take)/gather | solution.py:57
  106.5 0.9 broadcast_select_fusion
  (25 shorter events, 1.3 us)
Async XLA Ops:
  0.0 51.9 %copy-start = (bf16[32,512]{1,0:T(8,128)(2,1)S(1)}, bf16[32,512]{1,0:T(8,128)(2,1)}, u32[]{:S(2)}) copy-start(bf16[32,512]{1,0:T(8,128)(2,1)} %param.8) | copy-start | bytes 98308
  0.0 32.9 %copy-start.2 = (bf16[1,128]{1,0:T(2,128)(2,1)S(1)}, bf16[1,128]{1,0:T(2,128)(2,1)}, u32[]{:S(2)}) copy-start(bf16[1,128]{1,0:T(2,128)(2,1)} %param.6) | copy-start | bytes 772
  0.0 33.7 %copy-start.1 = (bf16[32,8,256]{2,1,0:T(8,128)(2,1)S(1)}, bf16[32,8,256]{2,1,0:T(8,128)(2,1)}, u32[]{:S(2)}) copy-start(bf16[32,8,256]{2,1,0:T(8,128)(2,1)} %param.7) | copy-start | bytes 393220
  11.5 34.4 %all-to-all-start = ((s32[128,4,2]{1,2,0:T(2,128)}), s32[128,4,2]{1,2,0:T(2,128)S(1)}, u32[]{:S(2)}, u32[]{:S(2)}) async-start(s32[128,4,2]{1,2,0:T(2,128)} %copy.19), calls=%async_computation | async-start | bytes 262144 | tf_op jit(solution)/shard_map/all_to_all | solution.py:40
  46.6 17.9 %all-to-all-start.1 = ((s32[128,4,2]{0,2,1:T(2,128)}), s32[128,4,2]{0,2,1:T(2,128)S(1)}, u32[]{:S(2)}, u32[]{:S(2)}) async-start(s32[128,4,2]{0,2,1:T(2,128)} %copy.20), calls=%async_computation.1 | async-start | bytes 8192 | tf_op jit(solution)/shard_map/all_to_all | solution.py:39
  69.1 22.8 %all-to-all-start.2 = ((bf16[128,4,2,128]{3,2,1,0:T(2,128)(2,1)}), bf16[128,4,2,128]{3,2,1,0:T(2,128)(2,1)S(1)}, u32[]{:S(2)}, u32[]{:S(2)}) async-start(bf16[128,4,2,128]{3,2,1,0:T(2,128)(2,1)} %bitcast.3), calls=%async_computation.2 | async-start | bytes 524288 | tf_op jit(solution)/shard_map/all_to_all | solution.py:50
  92.8 10.3 %all-to-all-start.3 = ((bf16[128,4,2,128]{3,2,0,1:T(2,128)(2,1)}), bf16[128,4,2,128]{3,2,0,1:T(2,128)(2,1)S(1)}, u32[]{:S(2)}, u32[]{:S(2)}) async-start(bf16[128,4,2,128]{3,2,0,1:T(2,128)(2,1)} %copy.26), calls=%async_computation.3 | async-start | bytes 524288 | tf_op jit(solution)/shard_map/all_to_all | solution.py:49
where the time goes:
time: 108 us; the launch traced here: 107 us
  starting transfers between devices  37.5 us (35%)
  waiting for transfers between devices  29.2 us (27%)
  local copies, waits for them, and re-layouts  28.1 us (26%)
  other arithmetic  12 us (11%)
    all_to_all x1, starting transfers between devices, on_device(): lax.all_to_all(wanted, 'blk', split_axis=0, concat_axis=0, tiled=True)  20.8 us
    all_to_all x1, waiting for transfers between devices, on_device(): lax.all_to_all(picked, 'blk', split_axis=0, concat_axis=0, tiled=True)  12.3 us
    all_to_all x1, waiting for transfers between devices, on_device(): lax.all_to_all(wanted, 'blk', split_axis=0, concat_axis=0, tiled=True)  11.9 us
    all_to_all x1, starting transfers between devices, on_device(): lax.all_to_all(picked, 'blk', split_axis=0, concat_axis=0, tiled=True)  6.17 us
    transpose x1, local copies, waits for them, and re-layouts, on_device(): products.reshape(middle_span, J1, J2, last_span, J3)  6.11 us
    reshape x1, local copies, waits for them, and re-layouts, on_device(): products.reshape(middle_span, J1, J2, last_span, J3)  5.89 us
    all_to_all x1, starting transfers between devices, on_device(): lax.all_to_all(lax.all_to_all(wanted, 'blk', split_axis=0, concat_axis=0,...  5.33 us
    all_to_all x1, starting transfers between devices, on_device(): lax.all_to_all(lax.all_to_all(picked, 'blk', split_axis=0, concat_axis=0,...  5.23 us
  transfers between devices with their start and end apart: 4, of which 3 were waited for; matrix products, arithmetic and copies ran while one was open for 17% of the time, Pallas kernels for 0%

commit v1 on v0

v1 whole, which is shorter than its diff:
```python
import jax
import jax.numpy as jnp
from jax import lax
from jax.experimental import pallas as pl
from jax.experimental.pallas import tpu as pltpu
from jax.sharding import PartitionSpec as P


R = 32
J1 = 4
J2 = 8
J3 = 4
W3 = 128
I2L = 8
GROUPS = 4
ROWS = 1024
KT = 256


def mid_last_kernel(zlo_ref, row_ref, mid_ref, last_ref, q_ref, w_ref, b_ref, y_ref):
    f32, bf16 = jnp.float32, jnp.bfloat16
    shape3 = (R, I2L, J2 * R)
    sub_i = lax.broadcasted_iota(jnp.int32, shape3, 1)
    lane_i = lax.broadcasted_iota(jnp.int32, shape3, 2)
    for t in range(GROUPS):
        x = mid_ref[pl.ds(t * 256, 256), :].astype(f32).reshape(shape3)
        for bit in range(3):
            rb = (sub_i >> bit) & 1
            lb = (lane_i >> (5 + bit)) & 1
            step, span = 1 << bit, R << bit
            up = pltpu.roll(pltpu.roll(x, 8 - step, 1), span, 2)
            down = pltpu.roll(pltpu.roll(x, step, 1), 256 - span, 2)
            x = jnp.where(rb == lb, x, jnp.where(rb == 0, up, down))
        w_ref[:, pl.ds(t * 256, 256)] = x.reshape(256, 256).astype(bf16)
    c_i = lax.broadcasted_iota(jnp.int32, (512, 512), 0)
    d_i = lax.broadcasted_iota(jnp.int32, (512, 512), 1)
    pick = jnp.where(c_i == (d_i & 127) * J3 + (d_i >> 7), 1.0, 0.0).astype(bf16)
    spread = jnp.dot(last_ref[...], pick, preferred_element_type=f32).astype(bf16)
    stacked = jnp.concatenate([spread[:, j * W3 : (j + 1) * W3] for j in range(J3)], axis=0)
    row = row_ref[...]
    i3 = row & (W3 - 1)
    hot3 = jnp.where(lax.broadcasted_iota(jnp.int32, (W3, ROWS), 0) == i3, 1.0, 0.0).astype(bf16)
    b_ref[...] = jnp.dot(stacked, hot3, preferred_element_type=f32).astype(bf16)
    group = (row >> 10) & 3
    slot = ((group & 1) << 1) | ((group >> 1) ^ zlo_ref[0])
    code_all = slot * I2L + ((row >> 7) & (I2L - 1))
    for kt in range(ROWS // KT):
        ks = pl.ds(kt * KT, KT)
        code = jnp.broadcast_to(code_all[:, kt * KT : (kt + 1) * KT], (R, KT))
        for c in range(GROUPS * I2L):
            mask = jnp.where(code == c, 1.0, 0.0).astype(bf16)
            for j in range(J3):
                y_ref[j, pl.ds(c * R, R), :] = b_ref[pl.ds(j * R, R), ks] * mask
        for j in range(J3):
            q_ref[j, :, ks] = jnp.dot(w_ref[...], y_ref[j], preferred_element_type=f32).astype(bf16)


def first_kernel(row_ref, first_ref, q_ref, out_ref, a_ref, t_ref):
    f32, bf16 = jnp.float32, jnp.bfloat16
    blocks = first_ref.shape[0]
    i1 = row_ref[...] >> 12
    hot1 = jnp.where(lax.broadcasted_iota(jnp.int32, (blocks, ROWS), 0) == i1, 1.0, 0.0).astype(bf16)
    a_ref[...] = lax.dot_general(
        first_ref[...], hot1, (((0,), (0,)), ((), ())), preferred_element_type=f32
    )

    def tile(kt, carry):
        ks = pl.ds(pl.multiple_of(kt * 128, 128), 128)
        acc = [[None] * J3 for _ in range(J1)]
        for r in range(0, R, 2):
            for j3 in range(J3):
                both = q_ref[j3, pl.ds(r * J2, 2 * J2), ks].astype(f32)
                for h in range(2):
                    q = both[h * J2 : (h + 1) * J2]
                    for j1 in range(J1):
                        term = a_ref[pl.ds(j1 * R + r + h, 1), ks] * q
                        acc[j1][j3] = term if acc[j1][j3] is None else acc[j1][j3] + term
        for j1 in range(J1):
            for j3 in range(J3):
                t_ref[pl.ds(j1 * J2 * J3 + j3, J2, stride=J3), :] = acc[j1][j3]
        out_ref[ks, :] = t_ref[...].T.astype(bf16)
        return carry

    lax.fori_loop(0, ROWS // 128, tile, 0)


def served_rows(first_core, middle_core, last_core, row_tt):
    blocks = lax.axis_size("blk")
    groups = lax.axis_size("sub")
    vmem = pl.BlockSpec(memory_space=pltpu.VMEM)
    row = row_tt.reshape(1, ROWS)
    zlo = (lax.axis_index("sub") // 2).astype(jnp.int32).reshape(1)
    mid = middle_core.reshape(R * I2L, J2 * R)
    other = lax.ppermute(mid, "sub", [(i, i ^ 2) for i in range(groups)])
    sent = jnp.broadcast_to(first_core, (blocks, J1 * R))
    first_all = lax.all_to_all(sent, "blk", split_axis=0, concat_axis=0, tiled=True)
    pair = jnp.concatenate([mid, other], axis=0)
    mid_all = lax.all_gather(pair, "sub", axis_index_groups=[[0, 1], [2, 3]], tiled=True)
    q = early_call(zlo, row, mid_all, last_core, vmem)
    return late_call(row, first_all, q, vmem)


def early_call(zlo, row, mid_all, last_core, vmem):
    return pl.pallas_call(
        mid_last_kernel,
        out_shape=jax.ShapeDtypeStruct((J3, R * J2, ROWS), jnp.bfloat16),
        in_specs=[pl.BlockSpec(memory_space=pltpu.SMEM), vmem, vmem, vmem],
        out_specs=vmem,
        scratch_shapes=[
            pltpu.VMEM((R * J2, GROUPS * I2L * R), jnp.bfloat16),
            pltpu.VMEM((J3 * R, ROWS), jnp.bfloat16),
            pltpu.VMEM((J3, GROUPS * I2L * R, KT), jnp.bfloat16),
        ],
        compiler_params=pltpu.CompilerParams(vmem_limit_bytes=24 * 1024 * 1024),
        name="mid_last",
    )(zlo, row, mid_all, last_core)


def late_call(row, first_all, q, vmem):
    return pl.pallas_call(
        first_kernel,
        out_shape=jax.ShapeDtypeStruct((ROWS, J1 * J2 * J3), jnp.bfloat16),
        in_specs=[vmem, vmem, vmem],
        out_specs=vmem,
        scratch_shapes=[
            pltpu.VMEM((J1 * R, ROWS), jnp.float32),
            pltpu.VMEM((J1 * J2 * J3, 128), jnp.float32),
        ],
        compiler_params=pltpu.CompilerParams(vmem_limit_bytes=24 * 1024 * 1024),
        name="first",
    )(row, first_all, q)


def solution(mesh):
    placed = (P("blk", None), P(None, "sub", None), P(), P(("blk", "sub")))
    return jax.shard_map(
        served_rows, mesh=mesh, in_specs=placed, out_specs=P(("blk", "sub"), None), check_vma=False
    )
```

time: 108 us -> 51.5 us (0.48)
  local copies, waits for them, and re-layouts: 28.1 us -> 2.77 us
  waiting for transfers between devices: 29.2 us -> 13.1 us
  starting transfers between devices: 37.5 us -> 23.9 us
  other arithmetic: 12 us -> 0.92 us
  Pallas kernels: 0 us -> 6.3 us
  blocking collectives: 0 us -> 4.19 us
    all_to_all x4 -> x1, starting transfers between devices: 37.5 us -> 19.1 us  [served_rows(): lax.all_to_all(sent, 'blk', split_axis=0, concat_axis=0, tiled=True)]
    all_to_all x4 -> x1, waiting for transfers between devices: 29.2 us -> 13.1 us  [served_rows(): lax.all_to_all(sent, 'blk', split_axis=0, concat_axis=0, tiled=True)]
    gather x3 -> x0, local copies, waits for them, and re-layouts: 10.9 us -> none  [the longest x1 4.52 us: on_device(): wanted = item_index[row_order].reshape(blocks, groups, per_peer)]
    sort x2 -> x0, other arithmetic: 8.73 us -> none  [the longest x1 4.37 us: on_device(): row_order = jnp.argsort(owners, stable=True)]
    reshape x8 -> x0, local copies, waits for them, and re-layouts: 8.33 us -> none  [the longest x1 5.89 us: on_device(): products.reshape(middle_span, J1, J2, last_span, J3)]
    pallas_call x0 -> x2, Pallas kernels: none -> 6.3 us  [the longest x1 3.16 us: early_call(): pl.pallas_call(mid_last_kernel, out_shape=jax.ShapeDtypeStruct((J3, R * J...]
    transpose x1 -> x0, local copies, waits for them, and re-layouts: 6.11 us -> none  [on_device(): products.reshape(middle_span, J1, J2, last_span, J3)]
    ppermute x0 -> x1, starting transfers between devices: none -> 4.81 us  [served_rows(): other = lax.ppermute(mid, 'sub', [(i, i ^ 2) for i in range(groups)])]
  transfers between devices with their start and end apart: 4 -> 2, of which waited for: 3 -> 1; matrix products, arithmetic and copies ran while one was open for 17% -> 3% of each run, Pallas kernels for 0% -> 0%
where the time goes in v1:
time: 51.5 us; the launch traced here: 51.2 us
  starting transfers between devices  23.9 us (46%)
  waiting for transfers between devices  13.1 us (25%)
  Pallas kernels  6.3 us (12%)
  blocking collectives  4.19 us (8%)
  local copies, waits for them, and re-layouts  2.77 us (5%)
  other arithmetic  0.92 us (2%)
    all_to_all x1, starting transfers between devices, served_rows(): lax.all_to_all(sent, 'blk', split_axis=0, concat_axis=0, tiled=True)  19.1 us
    all_to_all x1, waiting for transfers between devices, served_rows(): lax.all_to_all(sent, 'blk', split_axis=0, concat_axis=0, tiled=True)  13.1 us
    ppermute x1, starting transfers between devices, served_rows(): other = lax.ppermute(mid, 'sub', [(i, i ^ 2) for i in range(groups)])  4.81 us
    all_gather x1, blocking collectives, served_rows(): lax.all_gather(pair, 'sub', axis_index_groups=[[0, 1], [2, 3]], tiled=True)  4.19 us
    pallas_call x1, Pallas kernels, early_call(): pl.pallas_call(mid_last_kernel, out_shape=jax.ShapeDtypeStruct((J3, R * J...  3.16 us
    pallas_call x1, Pallas kernels, late_call(): pl.pallas_call(first_kernel, out_shape=jax.ShapeDtypeStruct((ROWS, J1 * J...  3.14 us
    unnamed x5, local copies, waits for them, and re-layouts  1.45 us
    broadcast_in_dim x1, local copies, waits for them, and re-layouts, served_rows(): sent = jnp.broadcast_to(first_core, (blocks, J1 * R))  1.32 us
  transfers between devices with their start and end apart: 2, of which 1 were waited for; matrix products, arithmetic and copies ran while one was open for 3% of the time, Pallas kernels for 0%

profile of v1, /device:TPU:1, one launch (start us, length us, event | category | flops | bytes accessed | tf_op | source)
XLA Modules:
  0.0 51.2 jit_solution(148729447527785594)
XLA Ops:
  0.0 4.8 %collective-permute-start = (bf16[256,256]{1,0:T(8,128)(2,1)}, bf16[256,256]{1,0:T(8,128)(2,1)S(1)}, u32[]{:S(2)}, u32[]{:S(2)}) collective-permute-start(bf16[256,256]{1,0:T(8,128)(2,1)} %bitcast.10), channel_id=1, source_target_pairs={{0,2},{1,3},{2,0},{3,1},{4,6},{5,7},{6,4},{7,5},{8,10},{9,11},{10,... | collective-permute-start | bytes 393224 | tf_op jit(solution)/shard_map/ppermute | solution.py:94
  4.8 1.3 %broadcast_in_dim.2 = bf16[128,1,128]{2,1,0:T(2,128)(2,1)} broadcast(bf16[128]{0:T(256)(128)(2,1)} %bitcast.12), dimensions={2} | broadcast | bytes 33024 | tf_op jit(solution)/shard_map/broadcast_in_dim | solution.py:95
  6.1 19.1 %all-to-all-start = ((bf16[128,1,128]{2,1,0:T(2,128)(2,1)}), bf16[128,1,128]{2,1,0:T(2,128)(2,1)S(1)}, u32[]{:S(2)}, u32[]{:S(2)}) async-start(bf16[128,1,128]{2,1,0:T(2,128)(2,1)} %broadcast_in_dim.2), calls=%async_computation | async-start | bytes 131072 | tf_op jit(solution)/shard_map/all_to_all | solution.py:96
  25.2 13.1 %all-to-all-done = bf16[128,1,128]{2,1,0:T(2,128)(2,1)S(1)} async-done(((bf16[128,1,128]{2,1,0:T(2,128)(2,1)}), bf16[128,1,128]{2,1,0:T(2,128)(2,1)S(1)}, u32[]{:S(2)}, u32[]{:S(2)}) %all-to-all-start) | async-done | bytes 32800 | tf_op jit(solution)/shard_map/all_to_all | solution.py:96
  38.3 0.0 collective-permute-done
  38.3 0.9 %pad_maximum_fusion = bf16[512,256]{1,0:T(8,128)(2,1)S(1)} fusion(bf16[256,256]{1,0:T(8,128)(2,1)S(1)} %collective-permute-done, bf16[256,256]{1,0:T(8,128)(2,1)} %bitcast.11), kind=kLoop, calls=%fused_computation | loop fusion | flops 524288 | bytes 524288 | tf_op jit(solution)/shard_map/concatenate | solution.py:97
  39.3 4.2 %all_gather.3.mid_ref = bf16[1024,256]{1,0:T(8,128)(2,1)S(1)} all-gather(bf16[512,256]{1,0:T(8,128)(2,1)S(1)} %pad_maximum_fusion), channel_id=1, replica_groups={{0,1},{2,3},{4,5},{6,7},{8,9},{10,11},{12,13},{14,15},{16,17},{18,19},{..., dimensions={0}, use_global_device_ids=true | all-gather | bytes 786432 | tf_op jit(solution)/shard_map/all_gather | solution.py:98
  43.5 0.0 copy-start
  43.5 0.8 %copy-done = bf16[32,512]{1,0:T(8,128)(2,1)S(1)} copy-done((bf16[32,512]{1,0:T(8,128)(2,1)S(1)}, bf16[32,512]{1,0:T(8,128)(2,1)}, u32[]{:S(2)}) %copy-start) | copy-done | bytes 32792
  44.2 0.0 copy-start.1
  44.2 0.7 %copy-done.1 = s32[1024]{0:T(1024)S(1)} copy-done((s32[1024]{0:T(1024)S(1)}, s32[1024]{0:T(1024)}, u32[]{:S(2)}) %copy-start.1) | copy-done | bytes 4120
  44.9 3.2 %mid_last.1.q_ref = bf16[4,256,1024]{2,1,0:T(8,128)(2,1)S(1)} custom-call(s32[1]{0:T(128)} %bitcast.2.zlo_ref, s32[1,1024]{1,0:T(1,128)S(1)} %bitcast.8, bf16[1024,256]{1,0:T(8,128)(2,1)S(1)} %all_gather.3.mid_ref, bf16[32,512]{1,0:T(8,128)(2,1)S(1)} %copy-done), custom_call_target="tpu_custom_call" | custom-call | tf_op jit(solution)/shard_map/mid_last/pallas_call | solution.py:104
  48.1 3.1 %first.1 = bf16[1024,128]{1,0:T(8,128)(2,1)} custom-call(s32[1,1024]{1,0:T(1,128)S(1)} %bitcast.9, bf16[128,128]{1,0:T(8,128)(2,1)S(1)} %bitcast.7, bf16[4,256,1024]{2,1,0:T(8,128)(2,1)S(1)} %mid_last.1.q_ref), custom_call_target="tpu_custom_call" | custom-call | tf_op jit(solution)/shard_map/first/pallas_call | solution.py:120
  (1 shorter events, 0.0 us)
Async XLA Ops:
  0.0 38.3 %collective-permute-start = (bf16[256,256]{1,0:T(8,128)(2,1)}, bf16[256,256]{1,0:T(8,128)(2,1)S(1)}, u32[]{:S(2)}, u32[]{:S(2)}) collective-permute-start(bf16[256,256]{1,0:T(8,128)(2,1)} %bitcast.10), channel_id=1, source_target_pairs={{0,2},{1,3},{2,0},{3,1},{4,6},{5,7},{6,4},{7,5},{8,10},{9,11},{10,... | collective-permute-start | bytes 393224 | tf_op jit(solution)/shard_map/ppermute | solution.py:94
  6.1 32.2 %all-to-all-start = ((bf16[128,1,128]{2,1,0:T(2,128)(2,1)}), bf16[128,1,128]{2,1,0:T(2,128)(2,1)S(1)}, u32[]{:S(2)}, u32[]{:S(2)}) async-start(bf16[128,1,128]{2,1,0:T(2,128)(2,1)} %broadcast_in_dim.2), calls=%async_computation | async-start | bytes 131072 | tf_op jit(solution)/shard_map/all_to_all | solution.py:96
  43.5 0.8 %copy-start = (bf16[32,512]{1,0:T(8,128)(2,1)S(1)}, bf16[32,512]{1,0:T(8,128)(2,1)}, u32[]{:S(2)}) copy-start(bf16[32,512]{1,0:T(8,128)(2,1)} %last_ref.1) | copy-start | bytes 98308
  44.2 0.7 %copy-start.1 = (s32[1024]{0:T(1024)S(1)}, s32[1024]{0:T(1024)}, u32[]{:S(2)}) copy-start(s32[1024]{0:T(1024)} %param.7) | copy-start | bytes 12292

commit v2 on v1

v2 whole, which is shorter than its diff:
```python
import jax
import jax.numpy as jnp
from jax import lax
from jax.experimental import pallas as pl
from jax.experimental.pallas import tpu as pltpu
from jax.sharding import PartitionSpec as P


R = 32
J1 = 4
J2 = 8
J3 = 4
W3 = 128
I2L = 8
GROUPS = 4
ROWS = 1024
KT = 256


def mid_last_kernel(row_hbm, mid_ref, last_hbm, q_ref, w_ref, b_ref, y_ref, row_ref, last_ref, sems):
    f32, bf16 = jnp.float32, jnp.bfloat16
    get_row = pltpu.make_async_copy(row_hbm, row_ref, sems.at[0])
    get_last = pltpu.make_async_copy(last_hbm, last_ref, sems.at[1])
    get_row.start()
    get_last.start()
    shape3 = (R, I2L, J2 * R)
    sub_i = lax.broadcasted_iota(jnp.int32, shape3, 1)
    lane_i = lax.broadcasted_iota(jnp.int32, shape3, 2)
    for t in range(GROUPS):
        x = mid_ref[pl.ds(t * 256, 256), :].astype(f32).reshape(shape3)
        for bit in range(3):
            rb = (sub_i >> bit) & 1
            lb = (lane_i >> (5 + bit)) & 1
            step, span = 1 << bit, R << bit
            up = pltpu.roll(pltpu.roll(x, 8 - step, 1), span, 2)
            down = pltpu.roll(pltpu.roll(x, step, 1), 256 - span, 2)
            x = jnp.where(rb == lb, x, jnp.where(rb == 0, up, down))
        w_ref[:, pl.ds(t * 256, 256)] = x.reshape(256, 256).astype(bf16)
    get_row.wait()
    get_last.wait()
    c_i = lax.broadcasted_iota(jnp.int32, (512, 512), 0)
    d_i = lax.broadcasted_iota(jnp.int32, (512, 512), 1)
    pick = jnp.where(c_i == (d_i & 127) * J3 + (d_i >> 7), 1.0, 0.0).astype(bf16)
    spread = jnp.dot(last_ref[...], pick, preferred_element_type=f32).astype(bf16)
    stacked = jnp.concatenate([spread[:, j * W3 : (j + 1) * W3] for j in range(J3)], axis=0)
    row = row_ref[...]
    i3 = row & (W3 - 1)
    hot3 = jnp.where(lax.broadcasted_iota(jnp.int32, (W3, ROWS), 0) == i3, 1.0, 0.0).astype(bf16)
    b_ref[...] = jnp.dot(stacked, hot3, preferred_element_type=f32).astype(bf16)
    code_all = (row >> 7) & (GROUPS * I2L - 1)
    for kt in range(ROWS // KT):
        ks = pl.ds(kt * KT, KT)
        code = jnp.broadcast_to(code_all[:, kt * KT : (kt + 1) * KT], (R, KT))
        for c in range(GROUPS * I2L):
            mask = jnp.where(code == c, 1.0, 0.0).astype(bf16)
            for j in range(J3):
                y_ref[j, pl.ds(c * R, R), :] = b_ref[pl.ds(j * R, R), ks] * mask
        for j in range(J3):
            q_ref[j, :, ks] = jnp.dot(w_ref[...], y_ref[j], preferred_element_type=f32).astype(bf16)


def first_kernel(row_ref, first_ref, q_ref, out_ref, a_ref, t_ref, o_ref, sem):
    f32, bf16 = jnp.float32, jnp.bfloat16
    blocks = first_ref.shape[0]
    i1 = row_ref[...] >> 12
    hot1 = jnp.where(lax.broadcasted_iota(jnp.int32, (blocks, ROWS), 0) == i1, 1.0, 0.0).astype(bf16)
    a_ref[...] = lax.dot_general(
        first_ref[...], hot1, (((0,), (0,)), ((), ())), preferred_element_type=f32
    )

    def put(kt):
        ks = pl.ds(kt * 128, 128)
        return pltpu.make_async_copy(o_ref.at[ks], out_ref.at[ks], sem.at[kt])

    def tiles(step, carry):
        for u in range(8):
            kt = step * 8 + u
            ks = pl.ds(kt * 128, 128)
            acc = [[None] * J3 for _ in range(J1)]
            for r in range(0, R, 2):
                for j3 in range(J3):
                    both = q_ref[j3, pl.ds(r * J2, 2 * J2), ks].astype(f32)
                    for h in range(2):
                        q = both[h * J2 : (h + 1) * J2]
                        for j1 in range(J1):
                            term = a_ref[pl.ds(j1 * R + r + h, 1), ks] * q
                            acc[j1][j3] = term if acc[j1][j3] is None else acc[j1][j3] + term
            for j1 in range(J1):
                for j3 in range(J3):
                    t_ref[u, pl.ds(j1 * J2 * J3 + j3, J2, stride=J3), :] = acc[j1][j3]
            o_ref[ks, :] = t_ref[u].T.astype(bf16)
            put(kt).start()
        return carry

    tiles(0, 0)
    for kt in range(ROWS // 128):
        put(kt).wait()


def served_rows(first_core, middle_core, last_core, row_tt):
    blocks = lax.axis_size("blk")
    vmem = pl.BlockSpec(memory_space=pltpu.VMEM)
    row = row_tt.reshape(1, ROWS)
    mid = middle_core.reshape(R * I2L, J2 * R)
    sent = jnp.broadcast_to(first_core, (blocks, J1 * R))
    first_all = lax.all_to_all(sent, "blk", split_axis=0, concat_axis=0, tiled=True)
    mid_all = lax.all_gather(mid, "sub", tiled=True)
    q = early_call(row, mid_all, last_core, vmem)
    return late_call(row, first_all, q, vmem)


def early_call(row, mid_all, last_core, vmem):
    anywhere = pl.BlockSpec(memory_space=pltpu.HBM)
    return pl.pallas_call(
        mid_last_kernel,
        out_shape=jax.ShapeDtypeStruct((J3, R * J2, ROWS), jnp.bfloat16),
        in_specs=[anywhere, vmem, anywhere],
        out_specs=vmem,
        scratch_shapes=[
            pltpu.VMEM((R * J2, GROUPS * I2L * R), jnp.bfloat16),
            pltpu.VMEM((J3 * R, ROWS), jnp.bfloat16),
            pltpu.VMEM((J3, GROUPS * I2L * R, KT), jnp.bfloat16),
            pltpu.VMEM((1, ROWS), jnp.int32),
            pltpu.VMEM((R, W3 * J3), jnp.bfloat16),
            pltpu.SemaphoreType.DMA((2,)),
        ],
        compiler_params=pltpu.CompilerParams(vmem_limit_bytes=24 * 1024 * 1024),
        name="mid_last",
    )(
        pltpu.with_memory_space_constraint(row, pltpu.HBM),
        mid_all,
        pltpu.with_memory_space_constraint(last_core, pltpu.HBM),
    )


def late_call(row, first_all, q, vmem):
    return pl.pallas_call(
        first_kernel,
        out_shape=jax.ShapeDtypeStruct((ROWS, J1 * J2 * J3), jnp.bfloat16),
        in_specs=[vmem, vmem, vmem],
        out_specs=pl.BlockSpec(memory_space=pl.ANY),
        scratch_shapes=[
            pltpu.VMEM((J1 * R, ROWS), jnp.float32),
            pltpu.VMEM((8, J1 * J2 * J3, 128), jnp.float32),
            pltpu.VMEM((ROWS, J1 * J2 * J3), jnp.bfloat16),
            pltpu.SemaphoreType.DMA((ROWS // 128,)),
        ],
        compiler_params=pltpu.CompilerParams(vmem_limit_bytes=24 * 1024 * 1024),
        name="first",
    )(row, first_all, q)


def solution(mesh):
    placed = (P("blk", None), P(None, "sub", None), P(), P(("blk", "sub")))
    return jax.shard_map(
        served_rows, mesh=mesh, in_specs=placed, out_specs=P(("blk", "sub"), None), check_vma=False
    )
```

time: 51.5 us -> 38.1 us (0.74)
  waiting for transfers between devices: 13.1 us -> 0.01 us
  blocking collectives: 4.19 us -> 9.01 us
  starting transfers between devices: 23.9 us -> 20.8 us
  local copies, waits for them, and re-layouts: 2.77 us -> 1.34 us
  other arithmetic: 0.92 us -> 0 us
    all_to_all x1, waiting for transfers between devices: 13.1 us -> 0.01 us  [served_rows(): lax.all_to_all(sent, 'blk', split_axis=0, concat_axis=0, tiled=True)]
    all_gather x1, blocking collectives: 4.19 us -> 9.01 us  [served_rows(): mid_all = lax.all_gather(mid, 'sub', tiled=True)]
    ppermute x1 -> x0, starting transfers between devices: 4.81 us -> none  [served_rows(): other = lax.ppermute(mid, 'sub', [(i, i ^ 2) for i in range(groups)])]
    all_to_all x1, starting transfers between devices: 19.1 us -> 20.8 us  [served_rows(): lax.all_to_all(sent, 'blk', split_axis=0, concat_axis=0, tiled=True)]
    unnamed x5 -> x3, local copies, waits for them, and re-layouts: 1.45 us -> 0.01 us
    pallas_call x1, Pallas kernels: 3.16 us -> 4.38 us  [early_call(): pl.pallas_call(mid_last_kernel, out_shape=jax.ShapeDtypeStruct((J3, R * J...]
    concatenate x1 -> x0, other arithmetic: 0.92 us -> none  [served_rows(): pair = jnp.concatenate([mid, other], axis=0)]
    pallas_call x1, Pallas kernels: 3.14 us -> 2.25 us  [late_call(): pl.pallas_call(first_kernel, out_shape=jax.ShapeDtypeStruct((ROWS, J1 * J...]
  transfers between devices with their start and end apart: 2 -> 1, of which waited for: 1 -> 0; matrix products, arithmetic and copies ran while one was open for 3% -> 0% of each run, Pallas kernels for 0% -> 12%
where the time goes in v2:
time: 38.1 us; the launch traced here: 37.8 us
  starting transfers between devices  20.8 us (55%)
  blocking collectives  9.01 us (24%)
  Pallas kernels  6.63 us (17%)
  local copies, waits for them, and re-layouts  1.34 us (4%)
    all_to_all x1, starting transfers between devices, served_rows(): lax.all_to_all(sent, 'blk', split_axis=0, concat_axis=0, tiled=True)  20.8 us
    all_gather x1, blocking collectives, served_rows(): mid_all = lax.all_gather(mid, 'sub', tiled=True)  9.01 us
    pallas_call x1, Pallas kernels, early_call(): pl.pallas_call(mid_last_kernel, out_shape=jax.ShapeDtypeStruct((J3, R * J...  4.38 us
    pallas_call x1, Pallas kernels, late_call(): pl.pallas_call(first_kernel, out_shape=jax.ShapeDtypeStruct((ROWS, J1 * J...  2.25 us
    broadcast_in_dim x1, local copies, waits for them, and re-layouts, served_rows(): sent = jnp.broadcast_to(first_core, (blocks, J1 * R))  1.33 us
  transfers between devices with their start and end apart: 1, of which 0 were waited for; matrix products, arithmetic and copies ran while one was open for 0% of the time, Pallas kernels for 12%

profile of v2, /device:TPU:1, one launch (start us, length us, event | category | flops | bytes accessed | tf_op | source)
XLA Modules:
  0.0 37.8 jit_solution(16176922717738172123)
XLA Ops:
  0.0 0.0 copy-start
  0.0 1.3 %broadcast_in_dim.2 = bf16[128,1,128]{2,1,0:T(2,128)(2,1)} broadcast(bf16[128]{0:T(256)(128)(2,1)} %bitcast.10), dimensions={2} | broadcast | bytes 33024 | tf_op jit(solution)/shard_map/broadcast_in_dim | solution.py:105
  1.3 20.8 %all-to-all-start = ((bf16[128,1,128]{2,1,0:T(2,128)(2,1)}), bf16[128,1,128]{2,1,0:T(2,128)(2,1)S(1)}, u32[]{:S(2)}, u32[]{:S(2)}) async-start(bf16[128,1,128]{2,1,0:T(2,128)(2,1)} %broadcast_in_dim.2), calls=%async_computation | async-start | bytes 131072 | tf_op jit(solution)/shard_map/all_to_all | solution.py:106
  22.1 9.0 %all_gather.3.mid_ref = bf16[1024,256]{1,0:T(8,128)(2,1)S(1)} all-gather(bf16[256,256]{1,0:T(8,128)(2,1)} %bitcast.9), channel_id=1, replica_groups=mesh['blk'=128,'sub'=4] {'sub'}, dimensions={0}, use_global_device_ids=true | all-gather | bytes 655360 | tf_op jit(solution)/shard_map/all_gather | solution.py:107
  31.1 4.4 %mid_last.1.q_ref = bf16[4,256,1024]{2,1,0:T(8,128)(2,1)S(1)} custom-call(s32[1,1024]{1,0:T(1,128)} %bitcast.7, bf16[1024,256]{1,0:T(8,128)(2,1)S(1)} %all_gather.3.mid_ref, bf16[32,512]{1,0:T(8,128)(2,1)} %last_hbm.1), custom_call_target="tpu_custom_call" | custom-call | tf_op jit(solution)/shard_map/mid_last/pallas_call | solution.py:114
  35.5 0.0 all-to-all-done
  35.6 0.0 copy-done
  35.6 2.2 %first.1 = bf16[1024,128]{1,0:T(8,128)(2,1)} custom-call(s32[1,1024]{1,0:T(1,128)S(1)} %bitcast.8, bf16[128,128]{1,0:T(8,128)(2,1)S(1)} %bitcast.6, bf16[4,256,1024]{2,1,0:T(8,128)(2,1)S(1)} %mid_last.1.q_ref), custom_call_target="tpu_custom_call" | custom-call | tf_op jit(solution)/shard_map/first/pallas_call | solution.py:137
  (1 shorter events, 0.0 us)
Async XLA Ops:
  0.0 35.6 %copy-start = (s32[1024]{0:T(1024)S(1)}, s32[1024]{0:T(1024)}, u32[]{:S(2)}) copy-start(s32[1024]{0:T(1024)} %param.7) | copy-start | bytes 12292
  1.3 34.2 %all-to-all-start = ((bf16[128,1,128]{2,1,0:T(2,128)(2,1)}), bf16[128,1,128]{2,1,0:T(2,128)(2,1)S(1)}, u32[]{:S(2)}, u32[]{:S(2)}) async-start(bf16[128,1,128]{2,1,0:T(2,128)(2,1)} %broadcast_in_dim.2), calls=%async_computation | async-start | bytes 131072 | tf_op jit(solution)/shard_map/all_to_all | solution.py:106

commit v3 on v2

--- a/solution.py
+++ b/solution.py
@@ -15,29 +15,32 @@
 GROUPS = 4
 ROWS = 1024
 KT = 256
-
-
-def mid_last_kernel(row_hbm, mid_ref, last_hbm, q_ref, w_ref, b_ref, y_ref, row_ref, last_ref, sems):
+LEAD = 75
+SOON = 6
+
+
+def mid_last_kernel(
+    order_ref, row_ref, mid_ref, last_ref, q_ref,
+    w_ref, b_ref, y_ref, x_ref, v_ref,
+):
     f32, bf16 = jnp.float32, jnp.bfloat16
-    get_row = pltpu.make_async_copy(row_hbm, row_ref, sems.at[0])
-    get_last = pltpu.make_async_copy(last_hbm, last_ref, sems.at[1])
-    get_row.start()
-    get_last.start()
-    shape3 = (R, I2L, J2 * R)
-    sub_i = lax.broadcasted_iota(jnp.int32, shape3, 1)
-    lane_i = lax.broadcasted_iota(jnp.int32, shape3, 2)
+    chunk = lax.broadcasted_iota(jnp.int32, (R, 128), 1) // R
     for t in range(GROUPS):
-        x = mid_ref[pl.ds(t * 256, 256), :].astype(f32).reshape(shape3)
-        for bit in range(3):
-            rb = (sub_i >> bit) & 1
-            lb = (lane_i >> (5 + bit)) & 1
-            step, span = 1 << bit, R << bit
-            up = pltpu.roll(pltpu.roll(x, 8 - step, 1), span, 2)
-            down = pltpu.roll(pltpu.roll(x, step, 1), 256 - span, 2)
-            x = jnp.where(rb == lb, x, jnp.where(rb == 0, up, down))
-        w_ref[:, pl.ds(t * 256, 256)] = x.reshape(256, 256).astype(bf16)
-    get_row.wait()
-    get_last.wait()
+        for hj in range(2):
+            x_ref[hj] = mid_ref[pl.ds(t * 256, 256), pl.ds(hj * 128, 128)].astype(f32)
+        for hi in range(2):
+            for hj in range(2):
+                turned = []
+                for i in range(4):
+                    v = x_ref[hj, pl.ds(hi * 4 + i, R, stride=I2L), :]
+                    turned.append([v] + [pltpu.roll(v, R * d, 1) for d in range(1, 4)])
+                for j in range(4):
+                    out = turned[0][(0 - j) % 4]
+                    for i in range(1, 4):
+                        out = jnp.where(chunk == i, turned[i][(i - j) % 4], out)
+                    v_ref[hi, pl.ds(hj * 4 + j, R, stride=J2), :] = out
+        for hi in range(2):
+            w_ref[:, pl.ds(t * 256 + hi * 128, 128)] = v_ref[hi].astype(bf16)
     c_i = lax.broadcasted_iota(jnp.int32, (512, 512), 0)
     d_i = lax.broadcasted_iota(jnp.int32, (512, 512), 1)
     pick = jnp.where(c_i == (d_i & 127) * J3 + (d_i >> 7), 1.0, 0.0).astype(bf16)
@@ -47,7 +50,10 @@
     i3 = row & (W3 - 1)
     hot3 = jnp.where(lax.broadcasted_iota(jnp.int32, (W3, ROWS), 0) == i3, 1.0, 0.0).astype(bf16)
     b_ref[...] = jnp.dot(stacked, hot3, preferred_element_type=f32).astype(bf16)
-    code_all = (row >> 7) & (GROUPS * I2L - 1)
+    group = (row >> 10) & 3
+    paired = ((group & 1) << 1) | ((group >> 1) ^ order_ref[1])
+    slot = jnp.where(order_ref[0] == 1, paired, group)
+    code_all = slot * I2L + ((row >> 7) & (I2L - 1))
     for kt in range(ROWS // KT):
         ks = pl.ds(kt * KT, KT)
         code = jnp.broadcast_to(code_all[:, kt * KT : (kt + 1) * KT], (R, KT))
@@ -62,7 +68,7 @@
 def first_kernel(row_ref, first_ref, q_ref, out_ref, a_ref, t_ref, o_ref, sem):
     f32, bf16 = jnp.float32, jnp.bfloat16
     blocks = first_ref.shape[0]
-    i1 = row_ref[...] >> 12
+    i1 = ((row_ref[...] >> 12) - LEAD) & (blocks - 1)
     hot1 = jnp.where(lax.broadcasted_iota(jnp.int32, (blocks, ROWS), 0) == i1, 1.0, 0.0).astype(bf16)
     a_ref[...] = lax.dot_general(
         first_ref[...], hot1, (((0,), (0,)), ((), ())), preferred_element_type=f32
@@ -97,40 +103,106 @@
         put(kt).wait()
 
 
+def stage_kernel(
+    first_hbm, row_hbm, last_hbm, mid_hbm, sent_hbm, row_ref, last_ref, mid_ref, one_ref, many_ref, sems
+):
+    one = pltpu.make_async_copy(first_hbm, one_ref, sems.at[0])
+    others = [
+        pltpu.make_async_copy(row_hbm, row_ref, sems.at[1]),
+        pltpu.make_async_copy(last_hbm, last_ref, sems.at[2]),
+        pltpu.make_async_copy(mid_hbm, mid_ref, sems.at[3]),
+    ]
+    one.start()
+    for copy in others:
+        copy.start()
+    one.wait()
+    many_ref[...] = jnp.broadcast_to(one_ref[...][None], many_ref.shape)
+    out = pltpu.make_async_copy(many_ref, sent_hbm, sems.at[4])
+    out.start()
+    for copy in others:
+        copy.wait()
+    out.wait()
+
+
+def stage_call(first_core, row, last_core, mid, blocks):
+    far = pl.BlockSpec(memory_space=pltpu.HBM)
+    vmem = pl.BlockSpec(memory_space=pltpu.VMEM)
+    i32, bf16 = jnp.int32, jnp.bfloat16
+    return pl.pallas_call(
+        stage_kernel,
+        out_shape=(
+            pltpu.HBM((blocks, 1, J1 * R), bf16),
+            pltpu.VMEM((1, ROWS), i32),
+            pltpu.VMEM((R, W3 * J3), bf16),
+            pltpu.VMEM((R * I2L, J2 * R), bf16),
+        ),
+        in_specs=[far] * 4,
+        out_specs=(far, vmem, vmem, vmem),
+        scratch_shapes=[
+            pltpu.VMEM((1, J1 * R), bf16),
+            pltpu.VMEM((blocks, 1, J1 * R), bf16),
+            pltpu.SemaphoreType.DMA((5,)),
+        ],
+        compiler_params=pltpu.CompilerParams(vmem_limit_bytes=4 * 1024 * 1024),
+        name="stage",
+    )(*[pltpu.with_memory_space_constraint(a, pltpu.HBM) for a in (first_core, row, last_core, mid)])
+
+
+def place_of(block):
+    return block // 16, (block // 4) % 4, block % 4
+
+
+def lateness(block):
+    y, _, z = place_of(block)
+    return 4 * z + jnp.minimum(y, 8 - y)
+
+
 def served_rows(first_core, middle_core, last_core, row_tt):
     blocks = lax.axis_size("blk")
     vmem = pl.BlockSpec(memory_space=pltpu.VMEM)
     row = row_tt.reshape(1, ROWS)
+    soon = lateness(lax.axis_index("blk")) <= SOON
+    zlo = lax.axis_index("sub") // 2
+    order = jnp.stack([soon.astype(jnp.int32), zlo.astype(jnp.int32)])
     mid = middle_core.reshape(R * I2L, J2 * R)
-    sent = jnp.broadcast_to(first_core, (blocks, J1 * R))
-    first_all = lax.all_to_all(sent, "blk", split_axis=0, concat_axis=0, tiled=True)
-    mid_all = lax.all_gather(mid, "sub", tiled=True)
-    q = early_call(row, mid_all, last_core, vmem)
+    early = [b for b in range(blocks) if 4 * (b % 4) + min(b // 16, 8 - b // 16) <= SOON]
+    pairs = [(4 * b + i, 4 * b + (i ^ 2)) for b in early for i in range(4)]
+    other = lax.ppermute(mid, ("blk", "sub"), pairs)
+    sent, row, last_near, mid_near = stage_call(first_core, row, last_core, mid, blocks)
+    ring = [[(p + LEAD) % blocks for p in range(blocks)]]
+    first_all = lax.all_to_all(
+        sent, "blk", split_axis=0, concat_axis=0, tiled=True, axis_index_groups=ring
+    ).reshape(blocks, J1 * R)
+    mid_all = lax.cond(soon, from_pair, from_four, mid_near, other)
+    q = early_call(order, row, mid_all, last_near, vmem)
     return late_call(row, first_all, q, vmem)
 
 
-def early_call(row, mid_all, last_core, vmem):
-    anywhere = pl.BlockSpec(memory_space=pltpu.HBM)
+def from_pair(mid, other):
+    pair = jnp.concatenate([mid, other], axis=0)
+    return lax.all_gather(pair, "sub", axis_index_groups=[[0, 1], [2, 3]], tiled=True)
+
+
+def from_four(mid, other):
+    return lax.all_gather(mid, "sub", tiled=True)
+
+
+def early_call(order, row, mid_all, last_core, vmem):
     return pl.pallas_call(
         mid_last_kernel,
         out_shape=jax.ShapeDtypeStruct((J3, R * J2, ROWS), jnp.bfloat16),
-        in_specs=[anywhere, vmem, anywhere],
+        in_specs=[pl.BlockSpec(memory_space=pltpu.SMEM), vmem, vmem, vmem],
         out_specs=vmem,
         scratch_shapes=[
             pltpu.VMEM((R * J2, GROUPS * I2L * R), jnp.bfloat16),
             pltpu.VMEM((J3 * R, ROWS), jnp.bfloat16),
             pltpu.VMEM((J3, GROUPS * I2L * R, KT), jnp.bfloat16),
-            pltpu.VMEM((1, ROWS), jnp.int32),
-            pltpu.VMEM((R, W3 * J3), jnp.bfloat16),
-            pltpu.SemaphoreType.DMA((2,)),
+            pltpu.VMEM((2, R * I2L, 128), jnp.float32),
+            pltpu.VMEM((2, R * J2, 128), jnp.float32),
         ],
         compiler_params=pltpu.CompilerParams(vmem_limit_bytes=24 * 1024 * 1024),
         name="mid_last",
-    )(
-        pltpu.with_memory_space_constraint(row, pltpu.HBM),
-        mid_all,
-        pltpu.with_memory_space_constraint(last_core, pltpu.HBM),
-    )
+    )(order, row, mid_all, last_core)
 
 
 def late_call(row, first_all, q, vmem):

time: 38.1 us -> 39.1 us (1.026)
  blocking collectives: 9.01 us -> 4.19 us
  waiting for transfers between devices: 0.01 us -> 3.49 us
  starting transfers between devices: 20.8 us -> 23.6 us
  local copies, waits for them, and re-layouts: 1.34 us -> 0.01 us
  Pallas kernels: 6.63 us -> 7.44 us
    all_gather x1, blocking collectives: 9.01 us -> 4.19 us  [from_pair(): lax.all_gather(pair, 'sub', axis_index_groups=[[0, 1], [2, 3]], tiled=True)]
    ppermute x0 -> x1, starting transfers between devices: none -> 4.81 us  [served_rows(): other = lax.ppermute(mid, ('blk', 'sub'), pairs)]
    all_to_all x1, waiting for transfers between devices: 0.01 us -> 3.49 us  [served_rows(): lax.all_to_all(sent, 'blk', split_axis=0, concat_axis=0, tiled=True, axis...]
    all_to_all x1, starting transfers between devices: 20.8 us -> 18.8 us  [served_rows(): lax.all_to_all(sent, 'blk', split_axis=0, concat_axis=0, tiled=True, axis...]
    pallas_call x0 -> x1, Pallas kernels: none -> 1.37 us  [stage_call(): pl.pallas_call(stage_kernel, out_shape=(pltpu.HBM((blocks, 1, J1 * R), bf...]
    broadcast_in_dim x1 -> x0, local copies, waits for them, and re-layouts: 1.33 us -> none  [served_rows(): sent = jnp.broadcast_to(first_core, (blocks, J1 * R))]
    pallas_call x1, Pallas kernels: 4.38 us -> 3.79 us  [early_call(): pl.pallas_call(mid_last_kernel, out_shape=jax.ShapeDtypeStruct((J3, R * J...]
  transfers between devices with their start and end apart: 1 -> 2, of which waited for: 0 -> 1; matrix products, arithmetic and copies ran while one was open for 0% -> 0% of each run, Pallas kernels for 12% -> 4%
where the time goes in v3:
time: 39.1 us; the launch traced here: 38.9 us
  starting transfers between devices  23.6 us (60%)
  Pallas kernels  7.44 us (19%)
  blocking collectives  4.19 us (11%)
  waiting for transfers between devices  3.49 us (9%)
    all_to_all x1, starting transfers between devices, served_rows(): lax.all_to_all(sent, 'blk', split_axis=0, concat_axis=0, tiled=True, axis...  18.8 us
    ppermute x1, starting transfers between devices, served_rows(): other = lax.ppermute(mid, ('blk', 'sub'), pairs)  4.81 us
    all_gather x1, blocking collectives, from_pair(): lax.all_gather(pair, 'sub', axis_index_groups=[[0, 1], [2, 3]], tiled=True)  4.19 us
    pallas_call x1, Pallas kernels, early_call(): pl.pallas_call(mid_last_kernel, out_shape=jax.ShapeDtypeStruct((J3, R * J...  3.79 us
    all_to_all x1, waiting for transfers between devices, served_rows(): lax.all_to_all(sent, 'blk', split_axis=0, concat_axis=0, tiled=True, axis...  3.49 us
    pallas_call x1, Pallas kernels, late_call(): pl.pallas_call(first_kernel, out_shape=jax.ShapeDtypeStruct((ROWS, J1 * J...  2.27 us
    pallas_call x1, Pallas kernels, stage_call(): pl.pallas_call(stage_kernel, out_shape=(pltpu.HBM((blocks, 1, J1 * R), bf...  1.37 us
  transfers between devices with their start and end apart: 2, of which 1 were waited for; matrix products, arithmetic and copies ran while one was open for 0% of the time, Pallas kernels for 4%

profile of v3, /device:TPU:1, one launch (start us, length us, event | category | flops | bytes accessed | tf_op | source)
XLA Modules:
  0.0 38.9 jit_solution(14499692831821044163)
XLA Ops:
  0.0 4.8 %collective-permute-start = (bf16[256,256]{1,0:T(8,128)(2,1)}, bf16[256,256]{1,0:T(8,128)(2,1)S(1)}, u32[]{:S(2)}, u32[]{:S(2)}) collective-permute-start(bf16[256,256]{1,0:T(8,128)(2,1)} %bitcast.8), channel_id=1, source_target_pairs={{0,2},{1,3},{2,0},{3,1},{4,6},{5,7},{6,4},{7,5},{16,18},{17,19},{1... | collective-permute-start | bytes 393224 | tf_op jit(solution)/shard_map/ppermute | solution.py:170
  4.8 1.4 %stage.1 = (bf16[128,1,128]{2,1,0:T(2,128)(2,1)}, s32[1,1024]{1,0:T(1,128)S(1)}, bf16[32,512]{1,0:T(8,128)(2,1)S(1)}, bf16[256,256]{1,0:T(8,128)(2,1)S(1)}) custom-call(bf16[1,128]{1,0:T(2,128)(2,1)} %first_hbm.1, s32[1,1024]{1,0:T(1,128)} %bitcast.10, bf16[32,512]{1,0:T(8,128)(2,1)} %last_hbm.1, bf16[256,256]{1,0:T(8,128)(2,1)} %bitcast.9), custom_call_target="tpu_custom_call" | custom-call | tf_op jit(solution)/shard_map/stage/pallas_call | solution.py:131
  6.2 18.8 %all-to-all-start = ((bf16[128,1,128]{2,1,0:T(2,128)(2,1)}), bf16[128,1,128]{2,1,0:T(2,128)(2,1)S(1)}, u32[]{:S(2)}, u32[]{:S(2)}) async-start(bf16[128,1,128]{2,1,0:T(2,128)(2,1)} %get-tuple-element.20), calls=%async_computation | async-start | bytes 131072 | tf_op jit(solution)/shard_map/all_to_all | solution.py:173
  25.0 0.1 pad_add_fusion.order_ref
  25.1 3.5 %all-to-all-done = bf16[128,1,128]{2,1,0:T(2,128)(2,1)S(1)} async-done(((bf16[128,1,128]{2,1,0:T(2,128)(2,1)}), bf16[128,1,128]{2,1,0:T(2,128)(2,1)S(1)}, u32[]{:S(2)}, u32[]{:S(2)}) %all-to-all-start) | async-done | bytes 32800 | tf_op jit(solution)/shard_map/all_to_all | solution.py:173
  28.6 0.0 collective-permute-done
  28.6 4.2 %conditional.1 = (bf16[1024,256]{1,0:T(8,128)(2,1)S(1)}) conditional(s32[]{:T(128)} %convert_element_type.4, bf16[256,256]{1,0:T(8,128)(2,1)S(1)} %get-tuple-element.21, (bf16[256,256]{1,0:T(8,128)(2,1)S(1)}, bf16[256,256]{1,0:T(8,128)(2,1)S(1)}) %tuple.11), branch_computations={%region_0.1_spmd, %region_1.2_spmd} | conditional | flops 524288 | bytes 1310728 | solution.py:176
  28.6 4.2 %all_gather.5 = bf16[1024,256]{1,0:T(8,128)(2,1)S(1)} all-gather(bf16[512,256]{1,0:T(8,128)(2,1)S(1)} %pad_maximum_fusion), channel_id=1, replica_groups={{0,1},{2,3},{4,5},{6,7},{8,9},{10,11},{12,13},{14,15},{16,17},{18,19},{..., dimensions={0}, use_global_device_ids=true | all-gather | bytes 786432 | tf_op jit(solution)/shard_map/cond/branch_1_fun/all_gather | solution.py:183
  32.8 3.8 %mid_last.1.q_ref = bf16[4,256,1024]{2,1,0:T(8,128)(2,1)S(1)} custom-call(s32[2]{0:T(128)S(1)} %pad_add_fusion.order_ref, s32[1,1024]{1,0:T(1,128)S(1)} %get-tuple-element.19.row_ref, bf16[1024,256]{1,0:T(8,128)(2,1)S(1)} %get-tuple-element.23.mid_ref, bf16[32,512]{1,0:T(8,128)(2,1)S(1)} %get-tuple-element.22.last_ref), custom_call_target="tpu_custom_call" | custom-call | tf_op jit(solution)/shard_map/mid_last/pallas_call | solution.py:191
  36.6 2.3 %first.1 = bf16[1024,128]{1,0:T(8,128)(2,1)} custom-call(s32[1,1024]{1,0:T(1,128)S(1)} %get-tuple-element.19.row_ref, bf16[128,128]{1,0:T(8,128)(2,1)S(1)} %bitcast.7, bf16[4,256,1024]{2,1,0:T(8,128)(2,1)S(1)} %mid_last.1.q_ref), custom_call_target="tpu_custom_call" | custom-call | tf_op jit(solution)/shard_map/first/pallas_call | solution.py:209
  (2 shorter events, 0.0 us)
Async XLA Ops:
  0.0 28.6 %collective-permute-start = (bf16[256,256]{1,0:T(8,128)(2,1)}, bf16[256,256]{1,0:T(8,128)(2,1)S(1)}, u32[]{:S(2)}, u32[]{:S(2)}) collective-permute-start(bf16[256,256]{1,0:T(8,128)(2,1)} %bitcast.8), channel_id=1, source_target_pairs={{0,2},{1,3},{2,0},{3,1},{4,6},{5,7},{6,4},{7,5},{16,18},{17,19},{1... | collective-permute-start | bytes 393224 | tf_op jit(solution)/shard_map/ppermute | solution.py:170
  6.2 22.4 %all-to-all-start = ((bf16[128,1,128]{2,1,0:T(2,128)(2,1)}), bf16[128,1,128]{2,1,0:T(2,128)(2,1)S(1)}, u32[]{:S(2)}, u32[]{:S(2)}) async-start(bf16[128,1,128]{2,1,0:T(2,128)(2,1)} %get-tuple-element.20), calls=%async_computation | async-start | bytes 131072 | tf_op jit(solution)/shard_map/all_to_all | solution.py:173

commit v4 on v3

--- a/solution.py
+++ b/solution.py
@@ -15,32 +15,21 @@
 GROUPS = 4
 ROWS = 1024
 KT = 256
-LEAD = 75
-SOON = 6
+LEAD = 17
+SOON = 7
+
+
+def rank_of(block):
+    return (((block + 1) & 3) << 5) | (((block >> 2) - LEAD) & 31)
 
 
 def mid_last_kernel(
     order_ref, row_ref, mid_ref, last_ref, q_ref,
-    w_ref, b_ref, y_ref, x_ref, v_ref,
+    w_ref, b_ref, y_ref,
 ):
     f32, bf16 = jnp.float32, jnp.bfloat16
-    chunk = lax.broadcasted_iota(jnp.int32, (R, 128), 1) // R
     for t in range(GROUPS):
-        for hj in range(2):
-            x_ref[hj] = mid_ref[pl.ds(t * 256, 256), pl.ds(hj * 128, 128)].astype(f32)
-        for hi in range(2):
-            for hj in range(2):
-                turned = []
-                for i in range(4):
-                    v = x_ref[hj, pl.ds(hi * 4 + i, R, stride=I2L), :]
-                    turned.append([v] + [pltpu.roll(v, R * d, 1) for d in range(1, 4)])
-                for j in range(4):
-                    out = turned[0][(0 - j) % 4]
-                    for i in range(1, 4):
-                        out = jnp.where(chunk == i, turned[i][(i - j) % 4], out)
-                    v_ref[hi, pl.ds(hj * 4 + j, R, stride=J2), :] = out
-        for hi in range(2):
-            w_ref[:, pl.ds(t * 256 + hi * 128, 128)] = v_ref[hi].astype(bf16)
+        w_ref[:, pl.ds(t * 256, 256)] = mid_ref[pl.ds(t * 256, 256), :]
     c_i = lax.broadcasted_iota(jnp.int32, (512, 512), 0)
     d_i = lax.broadcasted_iota(jnp.int32, (512, 512), 1)
     pick = jnp.where(c_i == (d_i & 127) * J3 + (d_i >> 7), 1.0, 0.0).astype(bf16)
@@ -68,7 +57,7 @@
 def first_kernel(row_ref, first_ref, q_ref, out_ref, a_ref, t_ref, o_ref, sem):
     f32, bf16 = jnp.float32, jnp.bfloat16
     blocks = first_ref.shape[0]
-    i1 = ((row_ref[...] >> 12) - LEAD) & (blocks - 1)
+    i1 = rank_of(row_ref[...] >> 12)
     hot1 = jnp.where(lax.broadcasted_iota(jnp.int32, (blocks, ROWS), 0) == i1, 1.0, 0.0).astype(bf16)
     a_ref[...] = lax.dot_general(
         first_ref[...], hot1, (((0,), (0,)), ((), ())), preferred_element_type=f32
@@ -104,13 +93,14 @@
 
 
 def stage_kernel(
-    first_hbm, row_hbm, last_hbm, mid_hbm, sent_hbm, row_ref, last_ref, mid_ref, one_ref, many_ref, sems
+    first_hbm, row_hbm, last_hbm, mid_hbm, sent_hbm, row_ref, last_ref, mid_ref,
+    one_ref, many_ref, raw_ref, x_ref, v_ref, sems,
 ):
     one = pltpu.make_async_copy(first_hbm, one_ref, sems.at[0])
     others = [
         pltpu.make_async_copy(row_hbm, row_ref, sems.at[1]),
         pltpu.make_async_copy(last_hbm, last_ref, sems.at[2]),
-        pltpu.make_async_copy(mid_hbm, mid_ref, sems.at[3]),
+        pltpu.make_async_copy(mid_hbm, raw_ref, sems.at[3]),
     ]
     one.start()
     for copy in others:
@@ -121,6 +111,22 @@
     out.start()
     for copy in others:
         copy.wait()
+    chunk = lax.broadcasted_iota(jnp.int32, (R, 128), 1) // R
+    for hj in range(2):
+        x_ref[hj] = raw_ref[:, pl.ds(hj * 128, 128)].astype(jnp.float32)
+    for hi in range(2):
+        for hj in range(2):
+            turned = []
+            for i in range(4):
+                v = x_ref[hj, pl.ds(hi * 4 + i, R, stride=I2L), :]
+                turned.append([v] + [pltpu.roll(v, R * d, 1) for d in range(1, 4)])
+            for j in range(4):
+                part = turned[0][(0 - j) % 4]
+                for i in range(1, 4):
+                    part = jnp.where(chunk == i, turned[i][(i - j) % 4], part)
+                v_ref[hi, pl.ds(hj * 4 + j, R, stride=J2), :] = part
+    for hi in range(2):
+        mid_ref[:, pl.ds(hi * 128, 128)] = v_ref[hi].astype(jnp.bfloat16)
     out.wait()
 
 
@@ -141,6 +147,9 @@
         scratch_shapes=[
             pltpu.VMEM((1, J1 * R), bf16),
             pltpu.VMEM((blocks, 1, J1 * R), bf16),
+            pltpu.VMEM((R * I2L, J2 * R), bf16),
+            pltpu.VMEM((2, R * I2L, 128), jnp.float32),
+            pltpu.VMEM((2, R * J2, 128), jnp.float32),
             pltpu.SemaphoreType.DMA((5,)),
         ],
         compiler_params=pltpu.CompilerParams(vmem_limit_bytes=4 * 1024 * 1024),
@@ -167,9 +176,9 @@
     mid = middle_core.reshape(R * I2L, J2 * R)
     early = [b for b in range(blocks) if 4 * (b % 4) + min(b // 16, 8 - b // 16) <= SOON]
     pairs = [(4 * b + i, 4 * b + (i ^ 2)) for b in early for i in range(4)]
-    other = lax.ppermute(mid, ("blk", "sub"), pairs)
     sent, row, last_near, mid_near = stage_call(first_core, row, last_core, mid, blocks)
-    ring = [[(p + LEAD) % blocks for p in range(blocks)]]
+    other = lax.ppermute(mid_near, ("blk", "sub"), pairs)
+    ring = [sorted(range(blocks), key=rank_of)]
     first_all = lax.all_to_all(
         sent, "blk", split_axis=0, concat_axis=0, tiled=True, axis_index_groups=ring
     ).reshape(blocks, J1 * R)
@@ -197,8 +206,6 @@
             pltpu.VMEM((R * J2, GROUPS * I2L * R), jnp.bfloat16),
             pltpu.VMEM((J3 * R, ROWS), jnp.bfloat16),
             pltpu.VMEM((J3, GROUPS * I2L * R, KT), jnp.bfloat16),
-            pltpu.VMEM((2, R * I2L, 128), jnp.float32),
-            pltpu.VMEM((2, R * J2, 128), jnp.float32),
         ],
         compiler_params=pltpu.CompilerParams(vmem_limit_bytes=24 * 1024 * 1024),
         name="mid_last",

time: 39.1 us -> 39.9 us (1.020)
  waiting for transfers between devices: 3.49 us -> 5.54 us
  starting transfers between devices: 23.6 us -> 22.9 us
  Pallas kernels: 7.44 us -> 6.88 us
    all_to_all x1, waiting for transfers between devices: 3.49 us -> 5.53 us  [served_rows(): lax.all_to_all(sent, 'blk', split_axis=0, concat_axis=0, tiled=True, axis...]
    all_to_all x1, starting transfers between devices: 18.8 us -> 18.1 us  [served_rows(): lax.all_to_all(sent, 'blk', split_axis=0, concat_axis=0, tiled=True, axis...]
    pallas_call x1, Pallas kernels: 3.79 us -> 3.23 us  [early_call(): pl.pallas_call(mid_last_kernel, out_shape=jax.ShapeDtypeStruct((J3, R * J...]
  transfers between devices with their start and end apart: 2 -> 2, of which waited for: 1 -> 1; matrix products, arithmetic and copies ran while one was open for 0% -> 0% of each run, Pallas kernels for 4% -> 0%
where the time goes in v4:
time: 39.9 us; the launch traced here: 39.7 us
  starting transfers between devices  22.9 us (57%)
  Pallas kernels  6.88 us (17%)
  waiting for transfers between devices  5.54 us (14%)
  blocking collectives  4.2 us (11%)
    all_to_all x1, starting transfers between devices, served_rows(): lax.all_to_all(sent, 'blk', split_axis=0, concat_axis=0, tiled=True, axis...  18.1 us
    all_to_all x1, waiting for transfers between devices, served_rows(): lax.all_to_all(sent, 'blk', split_axis=0, concat_axis=0, tiled=True, axis...  5.53 us
    ppermute x1, starting transfers between devices, served_rows(): other = lax.ppermute(mid_near, ('blk', 'sub'), pairs)  4.82 us
    all_gather x1, blocking collectives, from_pair(): lax.all_gather(pair, 'sub', axis_index_groups=[[0, 1], [2, 3]], tiled=True)  4.2 us
    pallas_call x1, Pallas kernels, early_call(): pl.pallas_call(mid_last_kernel, out_shape=jax.ShapeDtypeStruct((J3, R * J...  3.23 us
    pallas_call x1, Pallas kernels, late_call(): pl.pallas_call(first_kernel, out_shape=jax.ShapeDtypeStruct((ROWS, J1 * J...  2.28 us
    pallas_call x1, Pallas kernels, stage_call(): pl.pallas_call(stage_kernel, out_shape=(pltpu.HBM((blocks, 1, J1 * R), bf...  1.37 us
  transfers between devices with their start and end apart: 2, of which 1 were waited for; matrix products, arithmetic and copies ran while one was open for 0% of the time, Pallas kernels for 0%

profile of v4, /device:TPU:1, one launch (start us, length us, event | category | flops | bytes accessed | tf_op | source)
XLA Modules:
  0.0 39.7 jit_solution(5553627522640473205)
XLA Ops:
  0.0 1.4 %stage.1 = (bf16[128,1,128]{2,1,0:T(2,128)(2,1)}, s32[1,1024]{1,0:T(1,128)S(1)}, bf16[32,512]{1,0:T(8,128)(2,1)S(1)}, bf16[256,256]{1,0:T(8,128)(2,1)S(1)}) custom-call(bf16[1,128]{1,0:T(2,128)(2,1)} %first_hbm.1, s32[1,1024]{1,0:T(1,128)} %bitcast.9, bf16[32,512]{1,0:T(8,128)(2,1)} %last_hbm.1, bf16[256,256]{1,0:T(8,128)(2,1)} %bitcast.8), custom_call_target="tpu_custom_call" | custom-call | tf_op jit(solution)/shard_map/stage/pallas_call | solution.py:137
  1.4 4.8 %collective-permute-start = (bf16[256,256]{1,0:T(8,128)(2,1)S(1)}, bf16[256,256]{1,0:T(8,128)(2,1)S(1)}, u32[]{:S(2)}, u32[]{:S(2)}) collective-permute-start(bf16[256,256]{1,0:T(8,128)(2,1)S(1)} %get-tuple-element.21), channel_id=1, source_target_pairs={{0,2},{1,3},{2,0},{3,1},{4,6},{5,7},{6,4},{7,5},{16,18},{17,19},{1... | collective-permute-start | bytes 393224 | tf_op jit(solution)/shard_map/ppermute | solution.py:180
  6.2 18.1 %all-to-all-start = ((bf16[128,1,128]{2,1,0:T(2,128)(2,1)}), bf16[128,1,128]{2,1,0:T(2,128)(2,1)S(1)}, u32[]{:S(2)}, u32[]{:S(2)}) async-start(bf16[128,1,128]{2,1,0:T(2,128)(2,1)} %get-tuple-element.20), calls=%async_computation | async-start | bytes 131072 | tf_op jit(solution)/shard_map/all_to_all | solution.py:182
  24.4 0.1 pad_add_fusion.order_ref
  24.4 5.5 %all-to-all-done = bf16[128,1,128]{2,1,0:T(2,128)(2,1)S(1)} async-done(((bf16[128,1,128]{2,1,0:T(2,128)(2,1)}), bf16[128,1,128]{2,1,0:T(2,128)(2,1)S(1)}, u32[]{:S(2)}, u32[]{:S(2)}) %all-to-all-start) | async-done | bytes 32800 | tf_op jit(solution)/shard_map/all_to_all | solution.py:182
  30.0 0.0 collective-permute-done
  30.0 4.2 %conditional.1 = (bf16[1024,256]{1,0:T(8,128)(2,1)S(1)}) conditional(s32[]{:T(128)} %convert_element_type.4, bf16[256,256]{1,0:T(8,128)(2,1)S(1)} %get-tuple-element.21, (bf16[256,256]{1,0:T(8,128)(2,1)S(1)}, bf16[256,256]{1,0:T(8,128)(2,1)S(1)}) %tuple.11), branch_computations={%region_0.1_spmd, %region_1.2_spmd} | conditional | flops 524288 | bytes 1310728 | solution.py:185
  30.0 4.2 %all_gather.5 = bf16[1024,256]{1,0:T(8,128)(2,1)S(1)} all-gather(bf16[512,256]{1,0:T(8,128)(2,1)S(1)} %pad_maximum_fusion), channel_id=1, replica_groups={{0,1},{2,3},{4,5},{6,7},{8,9},{10,11},{12,13},{14,15},{16,17},{18,19},{..., dimensions={0}, use_global_device_ids=true | all-gather | bytes 786432 | tf_op jit(solution)/shard_map/cond/branch_1_fun/all_gather | solution.py:192
  34.2 3.2 %mid_last.1.q_ref = bf16[4,256,1024]{2,1,0:T(8,128)(2,1)S(1)} custom-call(s32[2]{0:T(128)S(1)} %pad_add_fusion.order_ref, s32[1,1024]{1,0:T(1,128)S(1)} %get-tuple-element.19.row_ref, bf16[1024,256]{1,0:T(8,128)(2,1)S(1)} %get-tuple-element.23.mid_ref, bf16[32,512]{1,0:T(8,128)(2,1)S(1)} %get-tuple-element.22.last_ref), custom_call_target="tpu_custom_call" | custom-call | tf_op jit(solution)/shard_map/mid_last/pallas_call | solution.py:200
  37.5 2.3 %first.1 = bf16[1024,128]{1,0:T(8,128)(2,1)} custom-call(s32[1,1024]{1,0:T(1,128)S(1)} %get-tuple-element.19.row_ref, bf16[128,128]{1,0:T(8,128)(2,1)S(1)} %bitcast.7, bf16[4,256,1024]{2,1,0:T(8,128)(2,1)S(1)} %mid_last.1.q_ref), custom_call_target="tpu_custom_call" | custom-call | tf_op jit(solution)/shard_map/first/pallas_call | solution.py:216
  (2 shorter events, 0.0 us)
Async XLA Ops:
  1.4 28.6 %collective-permute-start = (bf16[256,256]{1,0:T(8,128)(2,1)S(1)}, bf16[256,256]{1,0:T(8,128)(2,1)S(1)}, u32[]{:S(2)}, u32[]{:S(2)}) collective-permute-start(bf16[256,256]{1,0:T(8,128)(2,1)S(1)} %get-tuple-element.21), channel_id=1, source_target_pairs={{0,2},{1,3},{2,0},{3,1},{4,6},{5,7},{6,4},{7,5},{16,18},{17,19},{1... | collective-permute-start | bytes 393224 | tf_op jit(solution)/shard_map/ppermute | solution.py:180
  6.2 23.8 %all-to-all-start = ((bf16[128,1,128]{2,1,0:T(2,128)(2,1)}), bf16[128,1,128]{2,1,0:T(2,128)(2,1)S(1)}, u32[]{:S(2)}, u32[]{:S(2)}) async-start(bf16[128,1,128]{2,1,0:T(2,128)(2,1)} %get-tuple-element.20), calls=%async_computation | async-start | bytes 131072 | tf_op jit(solution)/shard_map/all_to_all | solution.py:182

commit v5 on v4

--- a/solution.py
+++ b/solution.py
@@ -30,15 +30,10 @@
     f32, bf16 = jnp.float32, jnp.bfloat16
     for t in range(GROUPS):
         w_ref[:, pl.ds(t * 256, 256)] = mid_ref[pl.ds(t * 256, 256), :]
-    c_i = lax.broadcasted_iota(jnp.int32, (512, 512), 0)
-    d_i = lax.broadcasted_iota(jnp.int32, (512, 512), 1)
-    pick = jnp.where(c_i == (d_i & 127) * J3 + (d_i >> 7), 1.0, 0.0).astype(bf16)
-    spread = jnp.dot(last_ref[...], pick, preferred_element_type=f32).astype(bf16)
-    stacked = jnp.concatenate([spread[:, j * W3 : (j + 1) * W3] for j in range(J3)], axis=0)
     row = row_ref[...]
     i3 = row & (W3 - 1)
     hot3 = jnp.where(lax.broadcasted_iota(jnp.int32, (W3, ROWS), 0) == i3, 1.0, 0.0).astype(bf16)
-    b_ref[...] = jnp.dot(stacked, hot3, preferred_element_type=f32).astype(bf16)
+    b_ref[...] = jnp.dot(last_ref[...], hot3, preferred_element_type=f32).astype(bf16)
     group = (row >> 10) & 3
     paired = ((group & 1) << 1) | ((group >> 1) ^ order_ref[1])
     slot = jnp.where(order_ref[0] == 1, paired, group)
@@ -94,23 +89,29 @@
 
 def stage_kernel(
     first_hbm, row_hbm, last_hbm, mid_hbm, sent_hbm, row_ref, last_ref, mid_ref,
-    one_ref, many_ref, raw_ref, x_ref, v_ref, sems,
+    one_ref, many_ref, raw_ref, raw_last_ref, pick_ref, x_ref, v_ref, sems,
 ):
     one = pltpu.make_async_copy(first_hbm, one_ref, sems.at[0])
     others = [
         pltpu.make_async_copy(row_hbm, row_ref, sems.at[1]),
-        pltpu.make_async_copy(last_hbm, last_ref, sems.at[2]),
+        pltpu.make_async_copy(last_hbm, raw_last_ref, sems.at[2]),
         pltpu.make_async_copy(mid_hbm, raw_ref, sems.at[3]),
     ]
     one.start()
     for copy in others:
         copy.start()
+    c_i = lax.broadcasted_iota(jnp.int32, (W3 * J3, W3 * J3), 0)
+    d_i = lax.broadcasted_iota(jnp.int32, (W3 * J3, W3 * J3), 1)
+    pick_ref[...] = jnp.where(c_i == (d_i & (W3 - 1)) * J3 + d_i // W3, 1.0, 0.0).astype(jnp.bfloat16)
     one.wait()
     many_ref[...] = jnp.broadcast_to(one_ref[...][None], many_ref.shape)
     out = pltpu.make_async_copy(many_ref, sent_hbm, sems.at[4])
     out.start()
     for copy in others:
         copy.wait()
+    spread = jnp.dot(raw_last_ref[...], pick_ref[...], preferred_element_type=jnp.float32)
+    for j in range(J3):
+        last_ref[pl.ds(j * R, R), :] = spread[:, j * W3 : (j + 1) * W3].astype(jnp.bfloat16)
     chunk = lax.broadcasted_iota(jnp.int32, (R, 128), 1) // R
     for hj in range(2):
         x_ref[hj] = raw_ref[:, pl.ds(hj * 128, 128)].astype(jnp.float32)
@@ -139,7 +140,7 @@
         out_shape=(
             pltpu.HBM((blocks, 1, J1 * R), bf16),
             pltpu.VMEM((1, ROWS), i32),
-            pltpu.VMEM((R, W3 * J3), bf16),
+            pltpu.VMEM((J3 * R, W3), bf16),
             pltpu.VMEM((R * I2L, J2 * R), bf16),
         ),
         in_specs=[far] * 4,
@@ -148,6 +149,8 @@
             pltpu.VMEM((1, J1 * R), bf16),
             pltpu.VMEM((blocks, 1, J1 * R), bf16),
             pltpu.VMEM((R * I2L, J2 * R), bf16),
+            pltpu.VMEM((R, W3 * J3), bf16),
+            pltpu.VMEM((W3 * J3, W3 * J3), bf16),
             pltpu.VMEM((2, R * I2L, 128), jnp.float32),
             pltpu.VMEM((2, R * J2, 128), jnp.float32),
             pltpu.SemaphoreType.DMA((5,)),

time: 39.9 us -> 39.7 us (level)
  no operation moved by 1% of the time
where the time goes in v5:
time: 39.7 us; the launch traced here: 39.6 us
  starting transfers between devices  22.9 us (58%)
  Pallas kernels  6.68 us (17%)
  waiting for transfers between devices  5.54 us (14%)
  blocking collectives  4.2 us (11%)
    all_to_all x1, starting transfers between devices, served_rows(): lax.all_to_all(sent, 'blk', split_axis=0, concat_axis=0, tiled=True, axis...  18.1 us
    all_to_all x1, waiting for transfers between devices, served_rows(): lax.all_to_all(sent, 'blk', split_axis=0, concat_axis=0, tiled=True, axis...  5.53 us
    ppermute x1, starting transfers between devices, served_rows(): other = lax.ppermute(mid_near, ('blk', 'sub'), pairs)  4.82 us
    all_gather x1, blocking collectives, from_pair(): lax.all_gather(pair, 'sub', axis_index_groups=[[0, 1], [2, 3]], tiled=True)  4.2 us
    pallas_call x1, Pallas kernels, early_call(): pl.pallas_call(mid_last_kernel, out_shape=jax.ShapeDtypeStruct((J3, R * J...  3.03 us
    pallas_call x1, Pallas kernels, late_call(): pl.pallas_call(first_kernel, out_shape=jax.ShapeDtypeStruct((ROWS, J1 * J...  2.27 us
    pallas_call x1, Pallas kernels, stage_call(): pl.pallas_call(stage_kernel, out_shape=(pltpu.HBM((blocks, 1, J1 * R), bf...  1.37 us
  transfers between devices with their start and end apart: 2, of which 1 were waited for; matrix products, arithmetic and copies ran while one was open for 0% of the time, Pallas kernels for 0%

profile of v5, /device:TPU:1, one launch (start us, length us, event | category | flops | bytes accessed | tf_op | source)
XLA Modules:
  0.0 39.6 jit_solution(16751478961668003309)
XLA Ops:
  0.0 1.4 %stage.1 = (bf16[128,1,128]{2,1,0:T(2,128)(2,1)}, s32[1,1024]{1,0:T(1,128)S(1)}, bf16[128,128]{1,0:T(8,128)(2,1)S(1)}, bf16[256,256]{1,0:T(8,128)(2,1)S(1)}) custom-call(bf16[1,128]{1,0:T(2,128)(2,1)} %first_hbm.1, s32[1,1024]{1,0:T(1,128)} %bitcast.9, bf16[32,512]{1,0:T(8,128)(2,1)} %last_hbm.1, bf16[256,256]{1,0:T(8,128)(2,1)} %bitcast.8), custom_call_target="tpu_custom_call" | custom-call | tf_op jit(solution)/shard_map/stage/pallas_call | solution.py:138
  1.4 4.8 %collective-permute-start = (bf16[256,256]{1,0:T(8,128)(2,1)S(1)}, bf16[256,256]{1,0:T(8,128)(2,1)S(1)}, u32[]{:S(2)}, u32[]{:S(2)}) collective-permute-start(bf16[256,256]{1,0:T(8,128)(2,1)S(1)} %get-tuple-element.21), channel_id=1, source_target_pairs={{0,2},{1,3},{2,0},{3,1},{4,6},{5,7},{6,4},{7,5},{16,18},{17,19},{1... | collective-permute-start | bytes 393224 | tf_op jit(solution)/shard_map/ppermute | solution.py:183
  6.2 18.1 %all-to-all-start = ((bf16[128,1,128]{2,1,0:T(2,128)(2,1)}), bf16[128,1,128]{2,1,0:T(2,128)(2,1)S(1)}, u32[]{:S(2)}, u32[]{:S(2)}) async-start(bf16[128,1,128]{2,1,0:T(2,128)(2,1)} %get-tuple-element.20), calls=%async_computation | async-start | bytes 131072 | tf_op jit(solution)/shard_map/all_to_all | solution.py:185
  24.4 0.1 pad_add_fusion.order_ref
  24.4 5.5 %all-to-all-done = bf16[128,1,128]{2,1,0:T(2,128)(2,1)S(1)} async-done(((bf16[128,1,128]{2,1,0:T(2,128)(2,1)}), bf16[128,1,128]{2,1,0:T(2,128)(2,1)S(1)}, u32[]{:S(2)}, u32[]{:S(2)}) %all-to-all-start) | async-done | bytes 32800 | tf_op jit(solution)/shard_map/all_to_all | solution.py:185
  30.0 0.0 collective-permute-done
  30.0 4.2 %conditional.1 = (bf16[1024,256]{1,0:T(8,128)(2,1)S(1)}) conditional(s32[]{:T(128)} %convert_element_type.4, bf16[256,256]{1,0:T(8,128)(2,1)S(1)} %get-tuple-element.21, (bf16[256,256]{1,0:T(8,128)(2,1)S(1)}, bf16[256,256]{1,0:T(8,128)(2,1)S(1)}) %tuple.11), branch_computations={%region_0.1_spmd, %region_1.2_spmd} | conditional | flops 524288 | bytes 1310728 | solution.py:188
  30.0 4.2 %all_gather.5 = bf16[1024,256]{1,0:T(8,128)(2,1)S(1)} all-gather(bf16[512,256]{1,0:T(8,128)(2,1)S(1)} %pad_maximum_fusion), channel_id=1, replica_groups={{0,1},{2,3},{4,5},{6,7},{8,9},{10,11},{12,13},{14,15},{16,17},{18,19},{..., dimensions={0}, use_global_device_ids=true | all-gather | bytes 786432 | tf_op jit(solution)/shard_map/cond/branch_1_fun/all_gather | solution.py:195
  34.2 3.0 %mid_last.1.q_ref = bf16[4,256,1024]{2,1,0:T(8,128)(2,1)S(1)} custom-call(s32[2]{0:T(128)S(1)} %pad_add_fusion.order_ref, s32[1,1024]{1,0:T(1,128)S(1)} %get-tuple-element.19.row_ref, bf16[1024,256]{1,0:T(8,128)(2,1)S(1)} %get-tuple-element.23.mid_ref, bf16[128,128]{1,0:T(8,128)(2,1)S(1)} %get-tuple-element.22.last_ref), custom_call_target="tpu_custom_call" | custom-call | tf_op jit(solution)/shard_map/mid_last/pallas_call | solution.py:203
  37.3 2.3 %first.1 = bf16[1024,128]{1,0:T(8,128)(2,1)} custom-call(s32[1,1024]{1,0:T(1,128)S(1)} %get-tuple-element.19.row_ref, bf16[128,128]{1,0:T(8,128)(2,1)S(1)} %bitcast.7, bf16[4,256,1024]{2,1,0:T(8,128)(2,1)S(1)} %mid_last.1.q_ref), custom_call_target="tpu_custom_call" | custom-call | tf_op jit(solution)/shard_map/first/pallas_call | solution.py:219
  (2 shorter events, 0.0 us)
Async XLA Ops:
  1.4 28.6 %collective-permute-start = (bf16[256,256]{1,0:T(8,128)(2,1)S(1)}, bf16[256,256]{1,0:T(8,128)(2,1)S(1)}, u32[]{:S(2)}, u32[]{:S(2)}) collective-permute-start(bf16[256,256]{1,0:T(8,128)(2,1)S(1)} %get-tuple-element.21), channel_id=1, source_target_pairs={{0,2},{1,3},{2,0},{3,1},{4,6},{5,7},{6,4},{7,5},{16,18},{17,19},{1... | collective-permute-start | bytes 393224 | tf_op jit(solution)/shard_map/ppermute | solution.py:183
  6.2 23.8 %all-to-all-start = ((bf16[128,1,128]{2,1,0:T(2,128)(2,1)}), bf16[128,1,128]{2,1,0:T(2,128)(2,1)S(1)}, u32[]{:S(2)}, u32[]{:S(2)}) async-start(bf16[128,1,128]{2,1,0:T(2,128)(2,1)} %get-tuple-element.20), calls=%async_computation | async-start | bytes 131072 | tf_op jit(solution)/shard_map/all_to_all | solution.py:185

commit v6 on v5

--- a/solution.py
+++ b/solution.py
@@ -35,8 +35,8 @@
     hot3 = jnp.where(lax.broadcasted_iota(jnp.int32, (W3, ROWS), 0) == i3, 1.0, 0.0).astype(bf16)
     b_ref[...] = jnp.dot(last_ref[...], hot3, preferred_element_type=f32).astype(bf16)
     group = (row >> 10) & 3
-    paired = ((group & 1) << 1) | ((group >> 1) ^ order_ref[1])
-    slot = jnp.where(order_ref[0] == 1, paired, group)
+    paired = ((group & 1) << 1) | ((group >> 1) ^ order_ref[1:2, :])
+    slot = jnp.where(order_ref[0:1, :] == 1, paired, group)
     code_all = slot * I2L + ((row >> 7) & (I2L - 1))
     for kt in range(ROWS // KT):
         ks = pl.ds(kt * KT, KT)
@@ -176,6 +176,7 @@
     soon = lateness(lax.axis_index("blk")) <= SOON
     zlo = lax.axis_index("sub") // 2
     order = jnp.stack([soon.astype(jnp.int32), zlo.astype(jnp.int32)])
+    order = jnp.broadcast_to(order[:, None], (2, ROWS))
     mid = middle_core.reshape(R * I2L, J2 * R)
     early = [b for b in range(blocks) if 4 * (b % 4) + min(b // 16, 8 - b // 16) <= SOON]
     pairs = [(4 * b + i, 4 * b + (i ^ 2)) for b in early for i in range(4)]
@@ -203,7 +204,7 @@
     return pl.pallas_call(
         mid_last_kernel,
         out_shape=jax.ShapeDtypeStruct((J3, R * J2, ROWS), jnp.bfloat16),
-        in_specs=[pl.BlockSpec(memory_space=pltpu.SMEM), vmem, vmem, vmem],
+        in_specs=[vmem, vmem, vmem, vmem],
         out_specs=vmem,
         scratch_shapes=[
             pltpu.VMEM((R * J2, GROUPS * I2L * R), jnp.bfloat16),

time: 39.7 us -> 39.3 us (0.990)
  Pallas kernels: 6.68 us -> 6.14 us
    pallas_call x1, Pallas kernels: 3.03 us -> 2.49 us  [early_call(): pl.pallas_call(mid_last_kernel, out_shape=jax.ShapeDtypeStruct((J3, R * J...]
where the time goes in v6:
time: 39.3 us; the launch traced here: 39.1 us
  starting transfers between devices  22.9 us (58%)
  Pallas kernels  6.14 us (16%)
  waiting for transfers between devices  5.54 us (14%)
  blocking collectives  4.2 us (11%)
    all_to_all x1, starting transfers between devices, served_rows(): lax.all_to_all(sent, 'blk', split_axis=0, concat_axis=0, tiled=True, axis...  18.1 us
    all_to_all x1, waiting for transfers between devices, served_rows(): lax.all_to_all(sent, 'blk', split_axis=0, concat_axis=0, tiled=True, axis...  5.53 us
    ppermute x1, starting transfers between devices, served_rows(): other = lax.ppermute(mid_near, ('blk', 'sub'), pairs)  4.82 us
    all_gather x1, blocking collectives, from_pair(): lax.all_gather(pair, 'sub', axis_index_groups=[[0, 1], [2, 3]], tiled=True)  4.2 us
    pallas_call x1, Pallas kernels, early_call(): pl.pallas_call(mid_last_kernel, out_shape=jax.ShapeDtypeStruct((J3, R * J...  2.49 us
    pallas_call x1, Pallas kernels, late_call(): pl.pallas_call(first_kernel, out_shape=jax.ShapeDtypeStruct((ROWS, J1 * J...  2.28 us
    pallas_call x1, Pallas kernels, stage_call(): pl.pallas_call(stage_kernel, out_shape=(pltpu.HBM((blocks, 1, J1 * R), bf...  1.37 us
  transfers between devices with their start and end apart: 2, of which 1 were waited for; matrix products, arithmetic and copies ran while one was open for 0% of the time, Pallas kernels for 0%

profile of v6, /device:TPU:1, one launch (start us, length us, event | category | flops | bytes accessed | tf_op | source)
XLA Modules:
  0.0 39.1 jit_solution(17990270666050154063)
XLA Ops:
  0.0 1.4 %stage.1 = (bf16[128,1,128]{2,1,0:T(2,128)(2,1)}, s32[1,1024]{1,0:T(1,128)S(1)}, bf16[128,128]{1,0:T(8,128)(2,1)S(1)}, bf16[256,256]{1,0:T(8,128)(2,1)S(1)}) custom-call(bf16[1,128]{1,0:T(2,128)(2,1)} %first_hbm.1, s32[1,1024]{1,0:T(1,128)} %bitcast.9, bf16[32,512]{1,0:T(8,128)(2,1)} %last_hbm.1, bf16[256,256]{1,0:T(8,128)(2,1)} %bitcast.8), custom_call_target="tpu_custom_call" | custom-call | tf_op jit(solution)/shard_map/stage/pallas_call | solution.py:138
  1.4 4.8 %collective-permute-start = (bf16[256,256]{1,0:T(8,128)(2,1)S(1)}, bf16[256,256]{1,0:T(8,128)(2,1)S(1)}, u32[]{:S(2)}, u32[]{:S(2)}) collective-permute-start(bf16[256,256]{1,0:T(8,128)(2,1)S(1)} %get-tuple-element.21), channel_id=1, source_target_pairs={{0,2},{1,3},{2,0},{3,1},{4,6},{5,7},{6,4},{7,5},{16,18},{17,19},{1... | collective-permute-start | bytes 393224 | tf_op jit(solution)/shard_map/ppermute | solution.py:184
  6.2 18.1 %all-to-all-start = ((bf16[128,1,128]{2,1,0:T(2,128)(2,1)}), bf16[128,1,128]{2,1,0:T(2,128)(2,1)S(1)}, u32[]{:S(2)}, u32[]{:S(2)}) async-start(bf16[128,1,128]{2,1,0:T(2,128)(2,1)} %get-tuple-element.20), calls=%async_computation | async-start | bytes 131072 | tf_op jit(solution)/shard_map/all_to_all | solution.py:186
  24.4 0.1 pad_add_fusion
  24.4 5.5 %all-to-all-done = bf16[128,1,128]{2,1,0:T(2,128)(2,1)S(1)} async-done(((bf16[128,1,128]{2,1,0:T(2,128)(2,1)}), bf16[128,1,128]{2,1,0:T(2,128)(2,1)S(1)}, u32[]{:S(2)}, u32[]{:S(2)}) %all-to-all-start) | async-done | bytes 32800 | tf_op jit(solution)/shard_map/all_to_all | solution.py:186
  30.0 0.0 collective-permute-done
  30.0 4.2 %conditional.1 = (bf16[1024,256]{1,0:T(8,128)(2,1)S(1)}) conditional(s32[]{:T(128)} %convert_element_type.4, bf16[256,256]{1,0:T(8,128)(2,1)S(1)} %get-tuple-element.21, (bf16[256,256]{1,0:T(8,128)(2,1)S(1)}, bf16[256,256]{1,0:T(8,128)(2,1)S(1)}) %tuple.11), branch_computations={%region_0.1_spmd, %region_1.2_spmd} | conditional | flops 524288 | bytes 1310728 | solution.py:189
  30.0 4.2 %all_gather.5 = bf16[1024,256]{1,0:T(8,128)(2,1)S(1)} all-gather(bf16[512,256]{1,0:T(8,128)(2,1)S(1)} %pad_maximum_fusion), channel_id=1, replica_groups={{0,1},{2,3},{4,5},{6,7},{8,9},{10,11},{12,13},{14,15},{16,17},{18,19},{..., dimensions={0}, use_global_device_ids=true | all-gather | bytes 786432 | tf_op jit(solution)/shard_map/cond/branch_1_fun/all_gather | solution.py:196
  34.2 0.1 broadcast_in_dim.2.order_ref
  34.3 2.5 %mid_last.1.q_ref = bf16[4,256,1024]{2,1,0:T(8,128)(2,1)S(1)} custom-call(s32[2,1024]{1,0:T(2,128)S(1)} %broadcast_in_dim.2.order_ref, s32[1,1024]{1,0:T(1,128)S(1)} %get-tuple-element.19.row_ref, bf16[1024,256]{1,0:T(8,128)(2,1)S(1)} %get-tuple-element.23.mid_ref, bf16[128,128]{1,0:T(8,128)(2,1)S(1)} %get-tuple-element.22.last_ref), custom_call_target="tpu_custom_call" | custom-call | tf_op jit(solution)/shard_map/mid_last/pallas_call | solution.py:204
  36.8 2.3 %first.1 = bf16[1024,128]{1,0:T(8,128)(2,1)} custom-call(s32[1,1024]{1,0:T(1,128)S(1)} %get-tuple-element.19.row_ref, bf16[128,128]{1,0:T(8,128)(2,1)S(1)} %bitcast.7, bf16[4,256,1024]{2,1,0:T(8,128)(2,1)S(1)} %mid_last.1.q_ref), custom_call_target="tpu_custom_call" | custom-call | tf_op jit(solution)/shard_map/first/pallas_call | solution.py:220
  (2 shorter events, 0.0 us)
Async XLA Ops:
  1.4 28.6 %collective-permute-start = (bf16[256,256]{1,0:T(8,128)(2,1)S(1)}, bf16[256,256]{1,0:T(8,128)(2,1)S(1)}, u32[]{:S(2)}, u32[]{:S(2)}) collective-permute-start(bf16[256,256]{1,0:T(8,128)(2,1)S(1)} %get-tuple-element.21), channel_id=1, source_target_pairs={{0,2},{1,3},{2,0},{3,1},{4,6},{5,7},{6,4},{7,5},{16,18},{17,19},{1... | collective-permute-start | bytes 393224 | tf_op jit(solution)/shard_map/ppermute | solution.py:184
  6.2 23.8 %all-to-all-start = ((bf16[128,1,128]{2,1,0:T(2,128)(2,1)}), bf16[128,1,128]{2,1,0:T(2,128)(2,1)S(1)}, u32[]{:S(2)}, u32[]{:S(2)}) async-start(bf16[128,1,128]{2,1,0:T(2,128)(2,1)} %get-tuple-element.20), calls=%async_computation | async-start | bytes 131072 | tf_op jit(solution)/shard_map/all_to_all | solution.py:186
